TPU v7x, 32 devices: a whole 2x2x4 slice. The times are simulated.
32 devices in a mesh: dp: 8 (over y, x, core), expert: 4 (over z).
Axes of the slice: x: 2, y: 2, z: 4, core: 2. Of those that a mesh axis runs over, the one named last changes fastest.
Arguments:
- tokens: bfloat16 [512, 2048], P('expert', 'dp'), may hold values from -6 to 6
- routes: int32 [512, 2], P('expert'), may hold values from 0 to 3, all different within a row
- dt_raw: float32 [512, 32], P('expert', 'dp'), may hold values from -5 to 5
- b_proj: float32 [512, 16], P('expert'), may hold values from -1.8 to 1.8
- c_proj: float32 [512, 16], P('expert'), may hold values from -1.8 to 1.8
- decay_rate: float32 [32], P('dp'), may hold values from 0.002 to 0.2
- skip_gain: float32 [32], P('dp'), may hold values from 0.5 to 1.5
- router_weight: float32 [2048, 4], P('dp'), may hold values from -0.125 to 0.125
- gate_weight: bfloat16 [4, 2048, 7168], P('expert', None, 'dp'), may hold values from -0.125 to 0.125
- up_weight: bfloat16 [4, 2048, 7168], P('expert', None, 'dp'), may hold values from -0.125 to 0.125
- down_weight: bfloat16 [4, 7168, 2048], P('expert', 'dp'), may hold values from -0.0625 to 0.0625
- out_grad: bfloat16 [512, 2048], P('expert', 'dp'), may hold values from -6 to 6
Outputs:
- block_out: bfloat16 [512, 2048], P('expert', 'dp')
- token_grad: bfloat16 [512, 2048], P('expert', 'dp')
- gate_grad: bfloat16 [4, 2048, 7168], P('expert', None, 'dp')
- up_grad: bfloat16 [4, 2048, 7168], P('expert', None, 'dp')
- down_grad: bfloat16 [4, 7168, 2048], P('expert', 'dp')
- router_grad: float32 [2048, 4], P('dp')
- rate_grad: float32 [32], P('dp')
- skip_grad: float32 [32], P('dp')
Inputs may be any that keep to these rules, and one draw needn't show every extreme that they name: `routes`: each token names two different experts.
All inputs are finite; a program needn't handle non-finite values.
Results may differ from a plain program's by a relative error of at most 0.02.
Values may be sent and summed in bfloat16 or wider, within the bound.
A program may use at most 64 MiB of HBM per device.

v0:
```python
import functools
import jax
import jax.numpy as jnp
from jax import lax
from jax.experimental import pallas as pl
from jax.experimental.pallas import tpu as pltpu
from jax.sharding import PartitionSpec as P


EPSILON = 1e-06
HIGHEST = lax.Precision.HIGHEST
MESH = pl.DeviceIdType.MESH


def loop(count, step):
    def run(i, carry):
        step(i)
        return carry

    lax.fori_loop(0, count, run, 0)


def greet(axes):
    barrier = pltpu.get_barrier_semaphore()
    total = 0
    for axis in axes:
        peers, place = (lax.axis_size(axis), lax.axis_index(axis))
        total += peers - 1

        def signal(k):
            pl.semaphore_signal(
                barrier, 1, device_id={axis: lax.rem(place + k + 1, peers)}, device_id_type=MESH
            )

        loop(peers - 1, signal)
    pl.semaphore_wait(barrier, total)


def swap_kernel(plan, *refs):
    amount = len(plan)
    ins, outs = (refs[:amount], refs[amount : 2 * amount])
    gathered = refs[2 * amount : 3 * amount]
    sends, recvs = (refs[3 * amount : 4 * amount], refs[4 * amount : 5 * amount])
    greet(sorted({axis for axis, _ in plan}))

    def copy_of(item, k):
        axis = plan[item][0]
        peers, place = (lax.axis_size(axis), lax.axis_index(axis))
        return pltpu.make_async_remote_copy(
            src_ref=ins[item],
            dst_ref=gathered[item].at[place],
            send_sem=sends[item].at[k],
            recv_sem=recvs[item].at[k],
            device_id={axis: lax.rem(place + k + 1, peers)},
            device_id_type=MESH,
        )

    for item, (axis, _) in enumerate(plan):
        loop(lax.axis_size(axis) - 1, lambda k: copy_of(item, k).start())
        gathered[item][lax.axis_index(axis)] = ins[item][...]
    for item, (axis, reduce) in enumerate(plan):
        peers, place = (lax.axis_size(axis), lax.axis_index(axis))

        def arrive(k):
            pltpu.make_async_remote_copy(
                src_ref=ins[item],
                dst_ref=gathered[item].at[lax.rem(place + peers - k - 1, peers)],
                send_sem=sends[item].at[k],
                recv_sem=recvs[item].at[k],
                device_id={axis: lax.rem(place + k + 1, peers)},
                device_id_type=MESH,
            ).wait()

        loop(peers - 1, arrive)
        if reduce:
            outs[item][...] = jnp.sum(gathered[item][...], axis=0)
        else:
            outs[item][...] = gathered[item][...]


def swap(name, number, *items):
    plan = tuple((axis, reduce) for _, axis, reduce in items)
    arrays = [array for array, _, _ in items]
    full = [(lax.axis_size(axis),) + array.shape for array, axis, _ in items]
    kept = [array.shape if reduce else shape for (array, _, reduce), shape in zip(items, full)]
    sems = [pltpu.SemaphoreType.DMA((shape[0] - 1,)) for shape in full]
    return pl.pallas_call(
        functools.partial(swap_kernel, plan),
        out_shape=[jax.ShapeDtypeStruct(shape, jnp.float32) for shape in kept],
        in_specs=[pl.BlockSpec(memory_space=pltpu.VMEM)] * len(items),
        out_specs=[pl.BlockSpec(memory_space=pltpu.VMEM)] * len(items),
        scratch_shapes=[pltpu.VMEM(shape, jnp.float32) for shape in full] + sems + sems,
        compiler_params=pltpu.CompilerParams(collective_id=number, has_side_effects=True),
        name=name,
    )(*arrays)


def running_sum(values):
    positions = jnp.arange(values.shape[0], dtype=jnp.int32)
    reached = (positions[:, None] >= positions[None, :]).astype(jnp.float32)
    return jnp.dot(reached, values, precision=HIGHEST)


def end_parts(normed, b_rows, dt_rows, decay_rate):
    steps_total = normed.shape[0]
    head_count = decay_rate.shape[0]
    step_size = jax.nn.softplus(dt_rows)
    running = running_sum(-step_size * decay_rate[None, :])
    tail_weight = jnp.exp(running[-1][None, :] - running) * step_size
    head_rows = normed.reshape(steps_total, head_count, -1)
    local_state = jnp.einsum("sh,shp,sn->hpn", tail_weight, head_rows, b_rows, precision=HIGHEST)
    return (jnp.exp(running[-1]), local_state.reshape(head_count, -1))


def ssd_piece(normed, b_rows, c_rows, dt_rows, decay_rate, skip_gain, state_start):
    steps_total = normed.shape[0]
    head_count = decay_rate.shape[0]
    state_width = b_rows.shape[1]
    step_size = jax.nn.softplus(dt_rows)
    running = running_sum(-step_size * decay_rate[None, :])
    positions = jnp.arange(steps_total, dtype=jnp.int32)
    causal = (positions[:, None] >= positions[None, :])[:, :, None]
    spread = jnp.where(causal, running[:, None, :] - running[None, :, :], 0.0)
    decay_table = jnp.where(causal, jnp.exp(spread), 0.0)
    pairing = jnp.dot(c_rows, b_rows.T, precision=HIGHEST)
    mixing = decay_table * pairing[:, :, None] * step_size[None, :, :]
    head_rows = normed.reshape(steps_total, head_count, -1)
    state_three = state_start.reshape(head_count, -1, state_width)
    mixed = jnp.einsum("tsh,shp->thp", mixing, head_rows, precision=HIGHEST)
    mixed = mixed + jnp.einsum(
        "tn,th,hpn->thp", c_rows, jnp.exp(running), state_three, precision=HIGHEST
    )
    mixed = mixed + skip_gain[None, :, None] * head_rows
    decay_total, local_state = end_parts(normed, b_rows, dt_rows, decay_rate)
    state_end = decay_total[:, None] * state_start + local_state
    return (mixed.reshape(steps_total, -1), state_end)


def carry_in(decays, states, reverse):
    peers, place = (lax.axis_size("expert"), lax.axis_index("expert"))
    held = jnp.zeros_like(states[0])
    for k in range(peers):
        at = peers - 1 - k if reverse else k
        reached = at > place if reverse else at < place
        held = jnp.where(reached, decays[at][:, None] * held + states[at], held)
    return held


def slices(total, width):
    return [(at, min(width, total - at)) for at in range(0, total, width)]


def expert_kernel(
    cap,
    send_rows,
    send_grads,
    gate_hbm,
    up_hbm,
    down_hbm,
    back_f,
    back_b,
    rows,
    grads,
    hidden,
    gate_back,
    up_back,
    gate_w,
    up_w,
    down_w,
    gate_s,
    up_s,
    away,
    mine,
    pair,
    chips,
    summed,
    z_send,
    z_recv,
    c_send,
    c_recv,
    p_send,
    p_recv,
    pair_send,
    pair_recv,
    chip_send,
    chip_recv,
    back_send,
    back_recv,
    local_sem,
    weight_sem,
):
    peers, place = (lax.axis_size("dp"), lax.axis_index("dp"))
    blocks, block = (lax.axis_size("expert"), lax.axis_index("expert"))
    chip_count = peers // 2
    chip, core = (place // 2, lax.rem(place, 2))
    partner = place + 1 - 2 * core
    width = send_rows.shape[1]
    units = gate_w.shape[1]
    sources = (send_rows, send_grads)
    wholes = (rows, grads)
    backs = (back_f, back_b)

    def strip(j):
        return pl.ds(pl.multiple_of(j * cap, 16), cap)

    def columns(d):
        return pl.ds(pl.multiple_of(d * width, 128), width)

    def ahead(k):
        return lax.rem(block + k, blocks)

    def chip_at(q):
        return lax.rem(chip + q, chip_count)

    weights = [
        pltpu.make_async_copy(hbm.at[0], held, weight_sem.at[n])
        for n, (hbm, held) in enumerate(
            ((gate_hbm, gate_w), (up_hbm, up_w), (down_hbm, down_w))
        )
    ]
    for item in weights:
        item.start()
    greet(("dp", "expert"))

    def own_copy(t):
        return pltpu.make_async_copy(
            sources[t].at[strip(block), :], wholes[t].at[strip(block), columns(place)], local_sem.at[t]
        )

    def z_copy(t, k, land):
        return pltpu.make_async_remote_copy(
            src_ref=sources[t].at[strip(ahead(k)), :],
            dst_ref=wholes[t].at[strip(land), columns(place)],
            send_sem=z_send.at[t, k],
            recv_sem=z_recv.at[t, k],
            device_id={"expert": ahead(k)},
            device_id_type=MESH,
        )

    def spread_copy(t, k, j, q, owner):
        cut = wholes[t].at[strip(j), columns(owner)]
        return pltpu.make_async_remote_copy(
            src_ref=cut,
            dst_ref=cut,
            send_sem=c_send.at[t, k * chip_count + q],
            recv_sem=c_recv.at[t, k * chip_count + q],
            device_id={"dp": 2 * chip_at(q) + core},
            device_id_type=MESH,
        )

    def partner_copy(t, k, j, q, owner):
        cut = wholes[t].at[strip(j), columns(owner)]
        return pltpu.make_async_remote_copy(
            src_ref=cut,
            dst_ref=cut,
            send_sem=p_send.at[t, k * chip_count + q],
            recv_sem=p_recv.at[t, k * chip_count + q],
            device_id={"dp": partner},
            device_id_type=MESH,
        )

    for t in range(2):
        own_copy(t).start()
        loop(blocks - 1, lambda k: z_copy(t, k + 1, block).start())

    def forward(t, k, j):
        loop(chip_count - 1, lambda q: spread_copy(t, k, j, q + 1, place).start())
        partner_copy(t, k, j, 0, place).start()

    for t in range(2):
        own_copy(t).wait()
        forward(t, 0, block)

        def pass_on(n):
            k = n + 1
            origin = lax.rem(block + blocks - k, blocks)
            z_copy(t, k, origin).wait_recv()
            forward(t, k, origin)

        loop(blocks - 1, pass_on)

    def origin_of(k):
        return lax.rem(block + blocks - k, blocks)

    def relay(t):
        def one(n):
            k, q = (n // (chip_count - 1), lax.rem(n, chip_count - 1) + 1)
            owner = 2 * lax.rem(chip + chip_count - q, chip_count) + core
            spread_copy(t, k, origin_of(k), q, owner).wait_recv()
            partner_copy(t, k, origin_of(k), q, owner).start()

        loop(blocks * (chip_count - 1), one)

        def last(n):
            k, q = (n // chip_count, lax.rem(n, chip_count))
            owner = 2 * lax.rem(chip + chip_count - q, chip_count) + 1 - core
            partner_copy(t, k, origin_of(k), q, owner).wait_recv()

        loop(blocks * chip_count, last)

    def pair_copy(t, c):
        return pltpu.make_async_remote_copy(
            src_ref=away.at[t, c],
            dst_ref=pair.at[t, c],
            send_sem=pair_send.at[t, c],
            recv_sem=pair_recv.at[t, c],
            device_id={"dp": partner},
            device_id_type=MESH,
        )

    def chip_copy(t, q):
        return pltpu.make_async_remote_copy(
            src_ref=mine.at[t, chip_at(q)],
            dst_ref=chips.at[t, q],
            send_sem=chip_send.at[t, q],
            recv_sem=chip_recv.at[t, q],
            device_id={"dp": 2 * chip_at(q) + core},
            device_id_type=MESH,
        )

    def back_copy(t, k, land):
        return pltpu.make_async_remote_copy(
            src_ref=summed.at[t, strip(ahead(k)), :],
            dst_ref=backs[t].at[strip(land), :],
            send_sem=back_send.at[t, k],
            recv_sem=back_recv.at[t, k],
            device_id={"expert": ahead(k)},
            device_id_type=MESH,
        )

    def tiles(t, term):
        def for_partner(q):
            c = chip_at(lax.rem(q + 1, chip_count))
            away[t, c] = term(2 * c + 1 - core).astype(jnp.bfloat16)
            pair_copy(t, c).start()

        loop(chip_count, for_partner)

        def for_mine(q):
            c = chip_at(lax.rem(q + 1, chip_count))
            value = term(2 * c + core)
            pair_copy(t, c).wait_recv()
            mine[t, c] = (value + pair[t, c].astype(jnp.float32)).astype(jnp.bfloat16)

            @pl.when(q < chip_count - 1)
            def _():
                chip_copy(t, q + 1).start()

        loop(chip_count, for_mine)

    def finish(t):
        total = mine[t, chip].astype(jnp.float32)
        for q in range(1, chip_count):
            chip_copy(t, q).wait_recv()
            total = total + chips[t, q].astype(jnp.float32)
        summed[t] = total.astype(jnp.bfloat16)
        loop(blocks - 1, lambda k: back_copy(t, k + 1, block).start())
        backs[t][strip(block), :] = summed[t, strip(block), :]

    relay(0)
    weights[0].wait()
    weights[1].wait()
    for at, span in slices(units, 256):
        cut = slice(at, at + span)
        gate = jnp.dot(rows[...], gate_w[:, cut], preferred_element_type=jnp.float32)
        up = jnp.dot(rows[...], up_w[:, cut], preferred_element_type=jnp.float32)
        gate_s[:, cut] = gate
        up_s[:, cut] = up
        hidden[:, cut] = (gate * jax.nn.sigmoid(gate) * up).astype(jnp.bfloat16)
    weights[2].wait()
    tiles(
        0,
        lambda d: jnp.dot(hidden[...], down_w[:, columns(d)], preferred_element_type=jnp.float32),
    )
    relay(1)
    nt = (((1,), (1,)), ((), ()))
    for at, span in slices(units, 256):
        cut = slice(at, at + span)
        unit_grad = lax.dot_general(
            grads[...], down_w[cut, :], nt, preferred_element_type=jnp.float32
        )
        gate = gate_s[:, cut]
        sigma = jax.nn.sigmoid(gate)
        gate_back[:, cut] = (
            unit_grad * up_s[:, cut] * sigma * (1.0 + gate * (1.0 - sigma))
        ).astype(jnp.bfloat16)
        up_back[:, cut] = (unit_grad * gate * sigma).astype(jnp.bfloat16)

    def input_term(d):
        at = pl.ds(pl.multiple_of(d * width, 128), width)
        first = lax.dot_general(
            gate_back[...], gate_w[at, :], nt, preferred_element_type=jnp.float32
        )
        return first + lax.dot_general(
            up_back[...], up_w[at, :], nt, preferred_element_type=jnp.float32
        )

    tiles(1, input_term)
    finish(0)
    finish(1)
    for t in range(2):

        def sent_back(n):
            copy = back_copy(t, n + 1, origin_of(n + 1))
            copy.wait_recv()
            copy.wait_send()
            z_copy(t, n + 1, block).wait_send()

        loop(blocks - 1, sent_back)
        loop(chip_count, lambda c: pair_copy(t, c).wait_send())
        loop(chip_count - 1, lambda q: chip_copy(t, q + 1).wait_send())

        def spread_done(n):
            k, q = (n // (chip_count - 1), lax.rem(n, chip_count - 1) + 1)
            spread_copy(t, k, origin_of(k), q, place).wait_send()

        loop(blocks * (chip_count - 1), spread_done)

        def partner_done(n):
            k, q = (n // chip_count, lax.rem(n, chip_count))
            partner_copy(t, k, origin_of(k), q, place).wait_send()

        loop(blocks * chip_count, partner_done)


def experts(cap, send_rows, send_grads, gate_weight, up_weight, down_weight):
    peers, blocks = (lax.axis_size("dp"), lax.axis_size("expert"))
    chip_count = peers // 2
    total, width = send_rows.shape
    features, units = gate_weight.shape[1:]
    half, full = (jnp.bfloat16, jnp.float32)
    vmem = pl.BlockSpec(memory_space=pltpu.VMEM)
    hbm = pl.BlockSpec(memory_space=pl.ANY)
    dma = pltpu.SemaphoreType.DMA
    shapes = [(total, width)] * 2 + [(total, features)] * 2 + [(total, units)] * 3
    return pl.pallas_call(
        functools.partial(expert_kernel, cap),
        out_shape=[jax.ShapeDtypeStruct(shape, half) for shape in shapes],
        in_specs=[vmem, vmem, hbm, hbm, hbm],
        out_specs=[vmem] * 7,
        scratch_shapes=[
            pltpu.VMEM((features, units), half),
            pltpu.VMEM((features, units), half),
            pltpu.VMEM((units, features), half),
            pltpu.VMEM((total, units), full),
            pltpu.VMEM((total, units), full),
            pltpu.VMEM((2, chip_count, total, width), half),
            pltpu.VMEM((2, chip_count, total, width), half),
            pltpu.VMEM((2, chip_count, total, width), half),
            pltpu.VMEM((2, chip_count, total, width), half),
            pltpu.VMEM((2, total, width), half),
            dma((2, blocks)),
            dma((2, blocks)),
            dma((2, blocks * chip_count)),
            dma((2, blocks * chip_count)),
            dma((2, blocks * chip_count)),
            dma((2, blocks * chip_count)),
            dma((2, chip_count)),
            dma((2, chip_count)),
            dma((2, chip_count)),
            dma((2, chip_count)),
            dma((2, blocks)),
            dma((2, blocks)),
            dma((2,)),
            dma((3,)),
        ],
        compiler_params=pltpu.CompilerParams(collective_id=7, has_side_effects=True),
        name="experts",
    )(send_rows, send_grads, gate_weight, up_weight, down_weight)


def body(
    tokens,
    routes,
    dt_raw,
    b_proj,
    c_proj,
    decay_rate,
    skip_gain,
    router_weight,
    gate_weight,
    up_weight,
    down_weight,
    out_grad,
):
    tok_count, width = tokens.shape
    expert_count = lax.axis_size("expert")
    features = width * lax.axis_size("dp")
    head_count = decay_rate.shape[0]
    capacity = 5 * tok_count // (2 * expert_count)
    padded = -(-capacity // 16) * 16
    inputs = tokens.astype(jnp.float32)
    (square_one,) = swap("sum_one", 1, (jnp.sum(inputs * inputs, axis=1)[None], "dp", True))
    scale_one = lax.rsqrt(square_one[0][:, None] / features + EPSILON)
    normed = inputs * scale_one
    decay_total, local_state = end_parts(normed, b_proj, dt_raw, decay_rate)
    state_width = local_state.shape[1]
    packed = jnp.concatenate(
        [local_state, jnp.broadcast_to(decay_total[:, None], (head_count, 128))], axis=1
    )
    (ends,) = swap("state_one", 2, (packed, "expert", False))
    decays = ends[:, :, state_width]
    state_in = carry_in(decays, ends[:, :, :state_width], False)

    def mixer(normed_in, rate_in, skip_in, state_start):
        return ssd_piece(normed_in, b_proj, c_proj, dt_raw, rate_in, skip_in, state_start)

    (mixed, state_end), mixer_pull = jax.vjp(mixer, normed, decay_rate, skip_gain, state_in)
    resid = (inputs + mixed).astype(jnp.bfloat16)
    resid_f = resid.astype(jnp.float32)
    raw_part = lax.dot_general(
        router_weight, resid_f, (((0,), (1,)), ((), ())), precision=HIGHEST
    )
    stats = jnp.concatenate([jnp.sum(resid_f * resid_f, axis=1)[None], raw_part], axis=0)
    (stats,) = swap("sum_two", 3, (stats, "dp", True))
    scale_row = lax.rsqrt(stats[0] / features + EPSILON)
    scale_two = scale_row[:, None]
    moe_in = (resid_f * scale_two).astype(jnp.bfloat16)
    expert_ids = jnp.arange(expert_count, dtype=jnp.int32)
    first_hot = (routes[:, 0:1] == expert_ids[None, :]).astype(jnp.float32)
    second_hot = (routes[:, 1:2] == expert_ids[None, :]).astype(jnp.float32)
    hot_gap = first_hot - second_hot
    raw_gap = jnp.sum(stats[1:].T * hot_gap, axis=1)
    logit_gap = raw_gap * scale_row
    first_weight = jax.nn.sigmoid(logit_gap)
    second_weight = jax.nn.sigmoid(-logit_gap)
    positions = jnp.arange(tok_count, dtype=jnp.int32)
    lower = (positions[:, None] > positions[None, :]).astype(jnp.bfloat16)
    both_hot = (first_hot + second_hot).astype(jnp.bfloat16)
    earlier = jnp.dot(lower, both_hot, preferred_element_type=jnp.float32)

    def slot_of(hot, ids):
        index = jnp.sum(earlier * hot, axis=1)
        target = ids.astype(jnp.float32) * padded + index
        return jnp.where(index < capacity, target, -1.0)

    slot_ids = jnp.arange(expert_count * padded, dtype=jnp.int32).astype(jnp.float32)[:, None]
    first_table = slot_ids == slot_of(first_hot, routes[:, 0])[None, :]
    second_table = slot_ids == slot_of(second_hot, routes[:, 1])[None, :]
    either = (first_table | second_table).astype(jnp.bfloat16)
    slot_weight = jnp.sum(
        jnp.where(first_table, first_weight[None, :], 0.0)
        + jnp.where(second_table, second_weight[None, :], 0.0),
        axis=1,
        keepdims=True,
    )
    send_rows = jnp.dot(either, moe_in, preferred_element_type=jnp.float32).astype(jnp.bfloat16)
    send_grads = jnp.dot(either, out_grad, preferred_element_type=jnp.float32) * slot_weight
    back_f, back_b, unit_rows, grad_rows, hidden, gate_back, up_back = experts(
        padded, send_rows, send_grads.astype(jnp.bfloat16), gate_weight, up_weight, down_weight
    )
    tn = (((0,), (0,)), ((), ()))
    down_part = lax.dot_general(hidden, grad_rows, tn, preferred_element_type=jnp.float32)
    gate_part = lax.dot_general(unit_rows, gate_back, tn, preferred_element_type=jnp.float32)
    up_part = lax.dot_general(unit_rows, up_back, tn, preferred_element_type=jnp.float32)
    pair_table = jnp.concatenate([first_table, second_table], axis=1).astype(jnp.bfloat16)
    per_slot = lax.dot_general(pair_table, back_f, tn, preferred_element_type=jnp.float32)
    first_out, second_out = (per_slot[:tok_count], per_slot[tok_count:])
    moe_sum = first_weight[:, None] * first_out + second_weight[:, None] * second_out
    block_out = (resid_f + moe_sum).astype(jnp.bfloat16)
    moe_grad = lax.dot_general(either, back_b, tn, preferred_element_type=jnp.float32)
    upstream = out_grad.astype(jnp.float32)
    inner_parts = jnp.stack(
        [
            jnp.sum(upstream * first_out, axis=1),
            jnp.sum(upstream * second_out, axis=1),
            jnp.sum(resid_f * moe_grad, axis=1),
        ]
    )
    (inner_all,) = swap("sum_three", 4, (inner_parts, "dp", True))
    gap_grad = first_weight * second_weight * (inner_all[0] - inner_all[1])
    inner = inner_all[2] + gap_grad * raw_gap
    logit_grad = gap_grad[:, None] * hot_gap
    moe_in_grad = moe_grad + jnp.dot(logit_grad, router_weight.T, precision=HIGHEST)
    router_part = lax.dot_general(logit_grad, moe_in.astype(jnp.float32), tn, precision=HIGHEST)
    resid_grad = (
        upstream
        + scale_two * moe_in_grad
        - resid_f * (scale_two * scale_two * scale_two) * (inner[:, None] / features)
    )
    running = running_sum(-jax.nn.softplus(dt_raw) * decay_rate[None, :])
    grad_heads = resid_grad.reshape(tok_count, head_count, -1)
    state_grad = jnp.einsum(
        "th,thp,tn->hpn", jnp.exp(running), grad_heads, c_proj, precision=HIGHEST
    ).reshape(head_count, -1)
    grad_ends, router_total = swap(
        "state_two", 5, (state_grad, "expert", False), (router_part, "expert", True)
    )
    later_grad = carry_in(decays, grad_ends, True)
    normed_grad, rate_part, skip_part, _ = mixer_pull((resid_grad, later_grad))
    inner_one = jnp.sum(normed_grad * inputs, axis=1)[None]
    small = jnp.pad(jnp.stack([rate_part, skip_part]), ((0, 0), (0, 128 - head_count)))
    inner_one, small = swap("sum_four", 6, (inner_one, "dp", True), (small, "expert", True))
    token_grad = (
        resid_grad
        + scale_one * normed_grad
        - inputs * (scale_one * scale_one * scale_one) * (inner_one[0][:, None] / features)
    )
    return (
        block_out,
        token_grad.astype(jnp.bfloat16),
        gate_part.astype(jnp.bfloat16)[None],
        up_part.astype(jnp.bfloat16)[None],
        down_part.astype(jnp.bfloat16)[None],
        router_total.T,
        small[0, :head_count],
        small[1, :head_count],
    )


def solution(mesh):
    return jax.shard_map(
        body,
        mesh=mesh,
        in_specs=(
            P("expert", "dp"),
            P("expert", None),
            P("expert", "dp"),
            P("expert", None),
            P("expert", None),
            P("dp"),
            P("dp"),
            P("dp", None),
            P("expert", None, "dp"),
            P("expert", None, "dp"),
            P("expert", "dp", None),
            P("expert", "dp"),
        ),
        out_specs=(
            P("expert", "dp"),
            P("expert", "dp"),
            P("expert", None, "dp"),
            P("expert", None, "dp"),
            P("expert", "dp", None),
            P("dp", None),
            P("dp"),
            P("dp"),
        ),
        check_vma=False,
    )
```

profile of v0, /device:TPU:0, one launch (start us, length us, event | category | flops | bytes accessed | tf_op | source)
XLA Modules:
  0.0 139.0 jit_solution(3272127288897134153)
XLA Ops:
  0.7 0.8 slice_bitcast_fusion.3
  1.5 0.9 fusion.63
  2.6 0.8 compare_select_fusion
  3.4 1.0 copy.52
  5.0 7.4 %sum_one.1 = f32[1,128]{1,0:T(1,128)} custom-call(f32[1,128]{1,0:T(1,128)} %bitcast.225), custom_call_target="tpu_custom_call" | custom-call | tf_op jit(solution)/shard_map/sum_one/pallas_call | solution.py:87
  13.8 1.0 fusion.128
  14.8 1.0 copy.55
  15.8 0.9 fusion.67
  17.4 7.6 %state_one.1 = f32[4,4,1152]{2,1,0:T(4,128)} custom-call(f32[4,1152]{1,0:T(4,128)} %pad_maximum_fusion.refs_0_), custom_call_target="tpu_custom_call" | custom-call | tf_op jit(solution)/shard_map/state_one/pallas_call | solution.py:87
  25.0 0.8 slice_reduce_fusion.3
  25.9 0.8 fusion.126
  27.2 0.9 convolution_bitcast_fusion.4
  28.2 1.3 fusion.9
  30.3 6.0 %sum_two.1 = f32[5,128]{1,0:T(8,128)} custom-call(f32[5,128]{1,0:T(8,128)} %pad_maximum_fusion.1.refs_0_), custom_call_target="tpu_custom_call" | custom-call | tf_op jit(solution)/shard_map/sum_two/pallas_call | solution.py:87
  37.0 0.8 select_reduce_fusion.1
  38.3 0.9 fusion.5.send_grads
  39.2 0.9 convolution_convert_fusion.send_rows
  40.1 49.2 %experts.1 = (bf16[320,256]{1,0:T(8,128)(2,1)}, bf16[320,256]{1,0:T(8,128)(2,1)}, bf16[320,2048]{1,0:T(8,128)(2,1)}, bf16[320,2048]{1,0:T(8,128)(2,1)}, bf16[320...) custom-call(bf16[320,256]{1,0:T(8,128)(2,1)} %convolution_convert_fusion.send_rows, ...), custom_call_target="tpu_custom_call" | custom-call | tf_op jit(solution)/shard_map/experts/pallas_call | solution.py:436
  89.4 1.3 fusion.19
  90.8 1.3 fusion.34
  92.6 5.9 %sum_three.1 = f32[3,128]{1,0:T(4,128)} custom-call(f32[3,128]{1,0:T(4,128)} %pad_maximum_fusion.2.refs_0_), custom_call_target="tpu_custom_call" | custom-call | tf_op jit(solution)/shard_map/sum_three/pallas_call | solution.py:87
  98.5 0.8 fusion.117
  99.8 0.8 fusion.60.refs_1_
  100.9 0.7 copy.65
  103.6 7.4 %state_two.1 = (f32[4,4,1024]{2,1,0:T(4,128)}, f32[4,256]{1,0:T(4,128)}) custom-call(f32[4,1024]{1,0:T(4,128)} %reshape.294.refs_0_, f32[4,256]{1,0:T(4,128)} %fusion.60.refs_1_), custom_call_target="tpu_custom_call" | custom-call | tf_op jit(solution)/shard_map/state_two/pallas_call | solution.py:87
  111.0 1.0 fusion.73
  112.2 0.8 fusion.127
  116.7 6.8 %sum_four.1 = (f32[1,128]{1,0:T(1,128)}, f32[2,128]{1,0:T(2,128)}) custom-call(f32[1,128]{1,0:T(1,128)} %bitcast.224, f32[2,128]{1,0:T(2,128)} %select_maximum_fusion.refs_1_), custom_call_target="tpu_custom_call" | custom-call | tf_op jit(solution)/shard_map/sum_four/pallas_call | solution.py:87
  124.9 1.2 slice_bitcast_fusion
  126.2 4.1 %convert_bitcast_fusion.2 = bf16[1,2048,896]{2,1,0:T(8,128)(2,1)} fusion(bf16[320,2048]{1,0:T(8,128)(2,1)S(1)} %copy-done.9, bf16[320,896]{1,0:T(8,128)(2,1)S(1)} %copy-done.12), kind=kOutput, calls=%fused_computation.2 | convolution fusion | flops 1176240128 | bytes 5554176 | tf_op jit(solution)/shard_map/dot_general | solution.py:554
  130.3 4.1 %convert_bitcast_fusion.1 = bf16[1,2048,896]{2,1,0:T(8,128)(2,1)} fusion(bf16[320,2048]{1,0:T(8,128)(2,1)S(1)} %copy-done.9, bf16[320,896]{1,0:T(8,128)(2,1)S(1)} %copy-done.11), kind=kOutput, calls=%fused_computation.1 | convolution fusion | flops 1176240128 | bytes 5554176 | tf_op jit(solution)/shard_map/dot_general | solution.py:555
  134.4 3.9 %convert_bitcast_fusion = bf16[1,896,2048]{2,1,0:T(8,128)(2,1)} fusion(bf16[320,896]{1,0:T(8,128)(2,1)S(1)} %copy-done.10, bf16[320,2048]{1,0:T(8,128)(2,1)S(1)} %copy-done.8), kind=kOutput, calls=%fused_computation | convolution fusion | flops 1176240128 | bytes 5554176 | tf_op jit(solution)/shard_map/dot_general | solution.py:553
  (84 shorter events, 14.7 us)
Async XLA Ops:
  0.6 29.0 %copy-start = (f32[256,4]{0,1:T(4,128)S(1)}, f32[256,4]{0,1:T(4,128)}, u32[]{:S(2)}) copy-start(f32[256,4]{0,1:T(4,128)} %param.19) | copy-start | bytes 12292
  0.6 37.6 %copy-start.4 = (bf16[128,256]{1,0:T(8,128)(2,1)S(1)}, bf16[128,256]{1,0:T(8,128)(2,1)}, u32[]{:S(2)}) copy-start(bf16[128,256]{1,0:T(8,128)(2,1)} %param.23) | copy-start | bytes 196612
  0.7 37.2 %copy-start.6 = (s32[128,2]{0,1:T(2,128)S(1)}, s32[128,2]{0,1:T(2,128)}, u32[]{:S(2)}) copy-start(s32[128,2]{0,1:T(2,128)} %param.13) | copy-start | bytes 3076
  40.1 60.5 %copy-start.2 = (f32[128,16]{0,1:T(8,128)S(1)}, f32[128,16]{0,1:T(8,128)}, u32[]{:S(2)}) copy-start(f32[128,16]{0,1:T(8,128)} %param.16) | copy-start | bytes 24580
  40.1 62.3 %copy-start.5 = (f32[128,4]{0,1:T(4,128)S(1)}, f32[128,4]{0,1:T(4,128)}, u32[]{:S(2)}) copy-start(f32[128,4]{0,1:T(4,128)} %param.14) | copy-start | bytes 6148
  89.3 21.7 %copy-start.1 = (f32[4,4,1152]{2,1,0:T(4,128)S(1)}, f32[4,4,1152]{2,1,0:T(4,128)}, u32[]{:S(2)}) copy-start(f32[4,4,1152]{2,1,0:T(4,128)} %state_one.1) | copy-start | bytes 221188
  89.3 24.2 %copy-start.3 = (f32[128,16]{0,1:T(8,128)S(1)}, f32[128,16]{0,1:T(8,128)}, u32[]{:S(2)}) copy-start(f32[128,16]{0,1:T(8,128)} %param.15) | copy-start | bytes 24580
  89.4 24.8 %copy-start.13 = (f32[4]{0:T(128)S(1)}, f32[4]{0:T(128)}, u32[]{:S(2)}) copy-start(f32[4]{0:T(128)} %param.18) | copy-start | bytes 52
  89.4 36.8 %copy-start.9 = (bf16[320,2048]{1,0:T(8,128)(2,1)S(1)}, bf16[320,2048]{1,0:T(8,128)(2,1)}, u32[]{:S(2)}) copy-start(bf16[320,2048]{1,0:T(8,128)(2,1)} %get-tuple-element.23) | copy-start | bytes 3932164
  89.4 36.8 %copy-start.12 = (bf16[320,896]{1,0:T(8,128)(2,1)S(1)}, bf16[320,896]{1,0:T(8,128)(2,1)}, u32[]{:S(2)}) copy-start(bf16[320,896]{1,0:T(8,128)(2,1)} %get-tuple-element.24) | copy-start | bytes 1720324
  126.2 4.1 %copy-start.11 = (bf16[320,896]{1,0:T(8,128)(2,1)S(1)}, bf16[320,896]{1,0:T(8,128)(2,1)}, u32[]{:S(2)}) copy-start(bf16[320,896]{1,0:T(8,128)(2,1)} %get-tuple-element.25) | copy-start | bytes 1720324
  130.3 4.1 %copy-start.8 = (bf16[320,2048]{1,0:T(8,128)(2,1)S(1)}, bf16[320,2048]{1,0:T(8,128)(2,1)}, u32[]{:S(2)}) copy-start(bf16[320,2048]{1,0:T(8,128)(2,1)} %get-tuple-element.27) | copy-start | bytes 3932164
  130.3 4.1 %copy-start.10 = (bf16[320,896]{1,0:T(8,128)(2,1)S(1)}, bf16[320,896]{1,0:T(8,128)(2,1)}, u32[]{:S(2)}) copy-start(bf16[320,896]{1,0:T(8,128)(2,1)} %get-tuple-element.26) | copy-start | bytes 1720324
  134.4 4.0 %copy-start.7 = (f32[4,256]{1,0:T(4,128)S(1)}, f32[4,256]{1,0:T(4,128)}, u32[]{:S(2)}) copy-start(f32[4,256]{1,0:T(4,128)} %get-tuple-element.28) | copy-start | bytes 12292
where the time goes:
time: 140 us; the launch traced here: 139 us
  Pallas kernels  90.3 us (64%)
  matrix products  26.9 us (19%)
  local copies, waits for them, and re-layouts  10.6 us (8%)
  other arithmetic  10 us (7%)
    pallas_call x1, Pallas kernels, experts(): pl.pallas_call(functools.partial(expert_kernel, cap), out_shape=[jax.Shap...  49.2 us
    pallas_call x6, Pallas kernels, swap(): pl.pallas_call(functools.partial(swap_kernel, plan), out_shape=[jax.Shape...  41.1 us
    dot_general x1, matrix products, body(): lax.dot_general(unit_rows, up_back, tn, preferred_element_type=jnp.float32)  4.12 us
    dot_general x1, matrix products, body(): lax.dot_general(unit_rows, gate_back, tn, preferred_element_type=jnp.floa...  4.1 us
    unnamed x33, local copies, waits for them, and re-layouts  4.05 us
    dot_general x1, matrix products, body(): lax.dot_general(hidden, grad_rows, tn, preferred_element_type=jnp.float32)  3.95 us

commit v1 on v0

v1 whole, which is shorter than its diff:
```python
import functools
import types
import jax
import jax.numpy as jnp
from jax import lax
from jax.experimental import pallas as pl
from jax.experimental.pallas import tpu as pltpu
from jax.sharding import PartitionSpec as P


EPSILON = 1e-06
HIGHEST = lax.Precision.HIGHEST
MESH = pl.DeviceIdType.MESH
DP, EXPERT = ("dp", "expert")
SEND, RECV, SRC, ALL = ("_send", "_recv", "_src", "_all")
HALF, FULL = (jnp.bfloat16, jnp.float32)
NN = (((1,), (0,)), ((), ()))
NT = (((1,), (1,)), ((), ()))
TN = (((0,), (0,)), ((), ()))


def loop(count, step):
    def run(i, carry):
        step(i)
        return carry

    lax.fori_loop(0, count, run, 0)


def slices(total, width):
    return [(at, min(width, total - at)) for at in range(0, total, width)]


def exact(a, b, dims=NN):
    return lax.dot_general(a, b, dims, precision=HIGHEST, preferred_element_type=FULL)


def fast(a, b, dims=NN):
    return lax.dot_general(a, b, dims, preferred_element_type=FULL)


def iota(shape, axis):
    return lax.broadcasted_iota(jnp.int32, shape, axis)


def softplus(v):
    return jnp.maximum(v, 0.0) + jnp.log(1.0 + jnp.exp(-jnp.abs(v)))


def sigmoid(v):
    return 1.0 / (1.0 + jnp.exp(-v))


def step_kernel(names, capacity, cap, fused, *refs):
    r = types.SimpleNamespace(**dict(zip(names, refs)))
    peers, place = (lax.axis_size(DP), lax.axis_index(DP))
    blocks, block = (lax.axis_size(EXPERT), lax.axis_index(EXPERT))
    chip_count = peers // 2
    chip, core = (place // 2, lax.rem(place, 2))
    partner = place + 1 - 2 * core
    count, width = r.tokens.shape
    features = width * peers
    heads = r.dt.shape[0]
    head_dim = width // heads
    experts = r.router.shape[0]
    units = r.down_w.shape[0]
    total = blocks * cap
    stat_rows = r.stat_src.shape[0]
    rows, grads = (r.rows, r.grads)
    sources, wholes = ((r.send_rows, r.send_grads), (rows, grads))
    away, mine, pair, chips = (r.away, r.mine, r.pair, r.chips)
    summed = r.summed
    backs = (r.back_f, r.back_b)
    down_w = r.down_w

    def strip(j):
        return pl.ds(pl.multiple_of(j * cap, 16), cap)

    def columns(d):
        return pl.ds(pl.multiple_of(d * width, 128), width)

    def ahead(k):
        return lax.rem(block + k, blocks)

    def origin_of(k):
        return lax.rem(block + blocks - k, blocks)

    def chip_at(q):
        return lax.rem(chip + q, chip_count)

    def chip_from(q):
        return lax.rem(chip + chip_count - q, chip_count)

    if fused:
        gu_w, gu_s = ((r.gu_w,), (r.gu_s,))
        gu_back, gu_back2 = ((r.gu_back,), (r.gu_back2,))
        halves = (r.gu_w.at[:, :units], r.gu_w.at[:, units:])

        def part(group, which, row, at, span):
            lo = at + which * units
            return group[0].at[row, lo : lo + span]
    else:
        gu_w, gu_s = ((r.gate_w, r.up_w), (r.gate_s, r.up_s))
        gu_back = (r.gate_back, r.up_back)
        gu_back2 = (r.gate_back2, r.up_back2)
        halves = (r.gate_w, r.up_w)

        def part(group, which, row, at, span):
            return group[which].at[row, at : at + span]

    weights = [
        pltpu.make_async_copy(hbm.at[0], held, r.weight_sem.at[n])
        for n, (hbm, held) in enumerate(
            ((r.down_hbm, down_w), (r.gate_hbm, halves[0]), (r.up_hbm, halves[1]))
        )
    ]
    for item in weights:
        item.start()

    barrier = pltpu.get_barrier_semaphore()
    for axis, amount, me in ((DP, peers, place), (EXPERT, blocks, block)):

        def signal(k):
            pl.semaphore_signal(
                barrier, 1, device_id={axis: lax.rem(me + k + 1, amount)}, device_id_type=MESH
            )

        loop(amount - 1, signal)

    def exchange(axis, src, land, sems):
        amount, me = (peers, place) if axis == DP else (blocks, block)
        send, recv = (getattr(r, sems + SEND), getattr(r, sems + RECV))

        def copy(k, at):
            return pltpu.make_async_remote_copy(
                src_ref=src(lax.rem(me + k, amount)),
                dst_ref=land(at),
                send_sem=send.at[k],
                recv_sem=recv.at[k],
                device_id={axis: lax.rem(me + k, amount)},
                device_id_type=MESH,
            )

        def start():
            loop(amount - 1, lambda k: copy(k + 1, me).start())

        def arrive():
            loop(
                amount - 1,
                lambda k: copy(k + 1, lax.rem(me + amount - k - 1, amount)).wait_recv(),
            )

        def sent():
            loop(amount - 1, lambda k: copy(k + 1, me).wait_send())

        return start, arrive, sent

    def shared(axis, name):
        src, everyone = (getattr(r, name + SRC), getattr(r, name + ALL))
        start, arrive, sent = exchange(
            axis, lambda _: src, lambda at: everyone.at[at], name
        )

        def launch(value):
            src[...] = value
            start()
            everyone[place if axis == DP else block] = value

        return launch, arrive, sent

    square_launch, square_arrive, square_sent = shared(DP, "square")
    decay_launch, decay_arrive, decay_sent = shared(EXPERT, "decay")
    state_launch, state_arrive, state_sent = shared(EXPERT, "state")
    stat_launch, stat_arrive, stat_sent = shared(DP, "stat")
    inner_launch, inner_arrive, inner_sent = shared(DP, "inner")
    sgrad_launch, sgrad_arrive, sgrad_sent = shared(EXPERT, "sgrad")
    router_launch, router_arrive, router_sent = shared(EXPERT, "rout")
    last_launch, last_arrive, last_sent = shared(DP, "last")
    small_launch, small_arrive, small_sent = shared(EXPERT, "small")
    slot_start, slot_arrive, slot_sent = exchange(
        EXPERT, lambda to: r.slot_src.at[to], lambda at: r.slot_all.at[at], "slot"
    )
    value_start, value_arrive, value_sent = exchange(
        EXPERT, lambda to: r.value_src.at[to], lambda at: r.value_all.at[at], "value"
    )

    def own_copy(t):
        return pltpu.make_async_copy(
            sources[t].at[strip(block), :],
            wholes[t].at[strip(block), columns(place)],
            r.local_sem.at[t],
        )

    def z_copy(t, k, land):
        return pltpu.make_async_remote_copy(
            src_ref=sources[t].at[strip(ahead(k)), :],
            dst_ref=wholes[t].at[strip(land), columns(place)],
            send_sem=r.z_send.at[t, k],
            recv_sem=r.z_recv.at[t, k],
            device_id={EXPERT: ahead(k)},
            device_id_type=MESH,
        )

    def spread_copy(t, k, j, q, owner):
        cut = wholes[t].at[strip(j), columns(owner)]
        return pltpu.make_async_remote_copy(
            src_ref=cut,
            dst_ref=cut,
            send_sem=r.c_send.at[t, k * chip_count + q],
            recv_sem=r.c_recv.at[t, k * chip_count + q],
            device_id={DP: 2 * chip_at(q) + core},
            device_id_type=MESH,
        )

    def partner_copy(t, k, j, q, owner):
        cut = wholes[t].at[strip(j), columns(owner)]
        return pltpu.make_async_remote_copy(
            src_ref=cut,
            dst_ref=cut,
            send_sem=r.p_send.at[t, k * chip_count + q],
            recv_sem=r.p_recv.at[t, k * chip_count + q],
            device_id={DP: partner},
            device_id_type=MESH,
        )

    def dispatch(t):
        own_copy(t).start()
        loop(blocks - 1, lambda k: z_copy(t, k + 1, block).start())

    def forward(t, k, j):
        loop(chip_count - 1, lambda q: spread_copy(t, k, j, q + 1, place).start())
        partner_copy(t, k, j, 0, place).start()

    def forward_own(t):
        own_copy(t).wait()
        forward(t, 0, block)

    def pass_on(t):
        def one(n):
            z_copy(t, n + 1, origin_of(n + 1)).wait_recv()
            forward(t, n + 1, origin_of(n + 1))

        loop(blocks - 1, one)

    def from_chip(t, q):
        owner = 2 * chip_from(q) + core

        def one(k):
            spread_copy(t, k, origin_of(k), q, owner).wait_recv()
            partner_copy(t, k, origin_of(k), q, owner).start()

        loop(blocks, one)

    def from_partner(t, q):
        owner = 2 * chip_from(q) + 1 - core
        loop(
            blocks, lambda k: partner_copy(t, k, origin_of(k), q, owner).wait_recv()
        )

    def pair_copy(t, c):
        return pltpu.make_async_remote_copy(
            src_ref=away.at[t, c],
            dst_ref=pair.at[t, c],
            send_sem=r.pair_send.at[t, c],
            recv_sem=r.pair_recv.at[t, c],
            device_id={DP: partner},
            device_id_type=MESH,
        )

    def chip_copy(t, q):
        return pltpu.make_async_remote_copy(
            src_ref=mine.at[t, chip_at(q)],
            dst_ref=chips.at[t, q],
            send_sem=r.chip_send.at[t, q],
            recv_sem=r.chip_recv.at[t, q],
            device_id={DP: 2 * chip_at(q) + core},
            device_id_type=MESH,
        )

    def back_copy(t, k, land):
        return pltpu.make_async_remote_copy(
            src_ref=summed.at[t, strip(ahead(k)), :],
            dst_ref=backs[t].at[strip(land), :],
            send_sem=r.back_send.at[t, k],
            recv_sem=r.back_recv.at[t, k],
            device_id={EXPERT: ahead(k)},
            device_id_type=MESH,
        )

    def tiles(t, term):
        def step(q):
            @pl.when(q < chip_count)
            def _():
                c = chip_at(lax.rem(q + 1, chip_count))
                away[t, c] = term(2 * c + 1 - core).astype(HALF)
                pair_copy(t, c).start()

            @pl.when(q > 0)
            def _():
                c = chip_at(lax.rem(q, chip_count))
                value = term(2 * c + core)
                pair_copy(t, c).wait_recv()
                mine[t, c] = (value + pair[t, c].astype(FULL)).astype(HALF)

                @pl.when(q < chip_count)
                def _():
                    chip_copy(t, q).start()

        loop(chip_count + 1, step)

    def finish(t):
        value = mine[t, chip].astype(FULL)
        for q in range(1, chip_count):
            chip_copy(t, q).wait_recv()
            value = value + chips[t, q].astype(FULL)
        summed[t] = value.astype(HALF)
        loop(blocks - 1, lambda k: back_copy(t, k + 1, block).start())
        backs[t][strip(block), :] = summed[t, strip(block), :]

    def backs_arrive(t):
        loop(
            blocks - 1, lambda n: back_copy(t, n + 1, origin_of(n + 1)).wait_recv()
        )

    inputs = r.tokens[...].astype(FULL)
    lane_head = iota((1, width), 1) // head_dim

    def spread_heads(cols):
        wide = jnp.zeros((cols.shape[0], width), FULL)
        for h in range(heads):
            wide = jnp.where(lane_head == h, cols[:, h : h + 1], wide)
        return wide

    ones_row = jnp.ones((8, width), FULL)
    square_part = exact(ones_row, inputs * inputs, NT)
    eye8 = (iota((8, 128), 0) == iota((8, 128), 1)).astype(FULL)
    eye_count = (iota((count, count), 0) == iota((count, count), 1)).astype(FULL)

    def to_columns(rows8):
        return exact(rows8, eye8, TN)

    pl.semaphore_wait(barrier, peers + blocks - 2)
    square_launch(square_part)

    routes_row = r.routes[...].astype(FULL)
    routes = exact(eye_count, routes_row, NT)
    expert_row = iota((stat_rows, count), 0).astype(FULL) - 1.0
    first_row = (routes_row[0:1, :] == expert_row).astype(FULL)
    second_row = (routes_row[1:2, :] == expert_row).astype(FULL)
    hot_gap_row = first_row - second_row
    expert_col = iota((count, experts), 1).astype(FULL)
    first_col = (routes[:, 0:1] == expert_col).astype(FULL)
    second_col = (routes[:, 1:2] == expert_col).astype(FULL)
    below = iota((count, count), 0) > iota((count, count), 1)
    above = (iota((count, count), 0) < iota((count, count), 1)).astype(HALF)
    earlier_row = fast((first_row + second_row).astype(HALF), above)
    earlier_col = fast(below.astype(HALF), (first_col + second_col).astype(HALF))

    def slot_of(earlier, hot, ids, axis):
        index = jnp.sum(earlier * hot, axis=axis, keepdims=True)
        return jnp.where(index < capacity, ids * cap + index, -1.0)

    slots_down = iota((total, count), 0).astype(FULL)
    slots_across = iota((count, total), 1).astype(FULL)
    first_table = slots_down == slot_of(earlier_row, first_row, routes_row[0:1, :], 0)
    second_table = slots_down == slot_of(earlier_row, second_row, routes_row[1:2, :], 0)
    first_back = slots_across == slot_of(earlier_col, first_col, routes[:, 0:1], 1)
    second_back = slots_across == slot_of(earlier_col, second_col, routes[:, 1:2], 1)
    either = (first_table | second_table).astype(HALF)
    r.table[:, :count] = first_table.astype(FULL)
    r.table[:, count:] = second_table.astype(FULL)
    r.across[:count, :] = first_back.astype(HALF)
    r.across[count:, :] = second_back.astype(HALF)

    r.send_grads[...] = fast(either, r.out_grad[...]).astype(HALF)
    dispatch(1)

    step_row = softplus(r.dt[...])
    step_col = exact(eye_count, step_row, NT)
    rate = r.rate[...]
    reached = jnp.where(below, 1.0, eye_count)
    sum_col = exact(reached, step_col)
    sum_row = exact(step_row, reached, NT)
    run_col = -sum_col * rate
    decay_end = jnp.exp(run_col[count - 1 : count, :])
    decay_wide = spread_heads(decay_end)
    decay_launch(jnp.broadcast_to(decay_wide, (8, width)))
    tail_col = jnp.exp(run_col[count - 1 : count, :] - run_col) * step_col
    tail_wide = spread_heads(tail_col)
    grow_wide = spread_heads(jnp.exp(run_col))
    skip_wide = spread_heads(r.skip[...])
    sum_wide = spread_heads(sum_col)
    b_side, c_side = (r.b_proj[...], r.c_proj[...])
    forward_own(1)

    square_arrive()
    scale_row_one = lax.rsqrt(jnp.sum(r.square_all[...], axis=0) / features + EPSILON)
    scale_one = to_columns(scale_row_one)[:, 0:1]
    normed = inputs * scale_one
    r.normed[...] = normed
    state_launch(exact(b_side, tail_wide * normed))

    causal = iota((count, count), 0) >= iota((count, count), 1)
    pairing = exact(c_side, b_side, TN)
    for h in range(heads):
        fall = run_col[:, h : h + 1] + sum_row[h : h + 1, :] * rate[0:1, h : h + 1]
        table = jnp.where(causal, jnp.exp(jnp.where(causal, fall, 0.0)), 0.0)
        r.mixing[:, h * count : (h + 1) * count] = table * pairing * step_row[h : h + 1, :]
        r.stack[h * count : (h + 1) * count, :] = jnp.where(lane_head == h, normed, 0.0)
    r.local[...] = exact(r.mixing[...], r.stack[...]) + skip_wide * normed
    pass_on(1)

    decay_arrive()
    state_arrive()

    def carry(states, reverse):
        held = jnp.zeros(r.state_src.shape, FULL)
        for k in range(blocks):
            at = blocks - 1 - k if reverse else k
            reach = at > block if reverse else at < block
            held = jnp.where(reach, r.decay_all[at][0:1, :] * held + states[at], held)
        return held

    state_in = carry(r.state_all, False)
    carried = grow_wide * exact(c_side, state_in, TN)
    r.carried[...] = carried
    resid = (inputs + (r.local[...] + carried)).astype(HALF)
    r.resid[...] = resid
    r.send_rows[...] = fast(either, resid).astype(HALF)
    dispatch(0)
    resid_f = resid.astype(FULL)
    eye_router = (iota((stat_rows, 128), 0) == iota((stat_rows, 128), 1) + 1).astype(FULL)
    router = r.router[...]
    router_row = exact(eye_router[:, :experts], router)
    squares = exact(ones_row[0:1], resid_f * resid_f, NT)
    stat_part = exact(router_row, resid_f, NT)
    stat_launch(jnp.where(iota((stat_rows, count), 0) == 0, squares, stat_part))
    forward_own(0)
    for q in range(1, chip_count):
        from_chip(1, q)

    stat_arrive()
    stats = jnp.sum(r.stat_all[...], axis=0)
    scale_row = lax.rsqrt(stats[0:1] / features + EPSILON)
    raw_gap = jnp.sum(stats * hot_gap_row, axis=0, keepdims=True)
    first_weight = sigmoid(raw_gap * scale_row)
    second_weight = sigmoid(-raw_gap * scale_row)
    pick8 = iota((8, 2 * count), 0)
    slot_rows = jnp.where(pick8 == 0, jnp.concatenate([first_weight, second_weight], axis=1), 0.0)
    slot_rows = jnp.where(pick8 == 1, jnp.concatenate([scale_row, scale_row], axis=1), slot_rows)
    r.slot_src[...] = jnp.zeros_like(r.slot_src)

    def fill_slot(e):
        r.slot_src[e, :, :cap] = exact(slot_rows, r.table[strip(e), :], NT)

    loop(blocks, fill_slot)
    slot_start()
    r.slot_all[block] = r.slot_src[block]
    pass_on(0)

    for q in range(chip_count):
        from_partner(1, q)
    weights[0].wait()
    for at, span in slices(units, 256):
        r.unit_raw[:, at : at + span] = fast(grads[...], down_w[at : at + span, :], NT)

    slot_arrive()
    pick = (iota((8, 256), 0) == iota((8, 256), 1) // 128).astype(FULL)

    def take_slots(j):
        wide = exact(r.slot_all[j], pick, TN)
        r.slot_weight[strip(j), :] = wide[:cap, :128]
        r.slot_scale[strip(j), :] = wide[:cap, 128:]

    loop(blocks, take_slots)

    weights[1].wait()
    weights[2].wait()
    for held in gu_s:
        held[...] = jnp.zeros_like(held)

    def chunk(d):
        for held, weight in zip(gu_s, gu_w):
            held[...] += fast(rows[:, columns(d)], weight[columns(d), :])

    def same_core(q):
        @pl.when(q > 0)
        def _():
            from_chip(0, q)

        chunk(2 * chip_from(q) + core)

    loop(chip_count, same_core)

    def other_core(q):
        from_partner(0, q)
        chunk(2 * chip_from(q) + 1 - core)

    loop(chip_count, other_core)

    tall = 16
    r.values[...] = jnp.zeros_like(r.values)

    def some_rows(i):
        row = pl.ds(pl.multiple_of(i * tall, tall), tall)
        scale = r.slot_scale[row, 0:1]
        weight = r.slot_weight[row, 0:1]
        first = jnp.zeros((tall, 1), FULL)
        second = jnp.zeros((tall, 1), FULL)
        for at, span in slices(units, 256):
            gate_raw = part(gu_s, 0, row, at, span)[...]
            up_raw = part(gu_s, 1, row, at, span)[...]
            unit_raw = r.unit_raw[row, at : at + span]
            gate, up = (gate_raw * scale, up_raw * scale)
            sigma = sigmoid(gate)
            silu = gate * sigma
            hid = silu * up
            unit = unit_raw * weight
            gate_b = unit * up * (sigma * (1.0 + gate * (1.0 - sigma)))
            up_b = unit * silu
            r.hidden[row, at : at + span] = hid.astype(HALF)
            r.hidden2[row, at : at + span] = (hid * weight).astype(HALF)
            part(gu_back, 0, row, at, span)[...] = gate_b.astype(HALF)
            part(gu_back, 1, row, at, span)[...] = up_b.astype(HALF)
            part(gu_back2, 0, row, at, span)[...] = (gate_b * scale).astype(HALF)
            part(gu_back2, 1, row, at, span)[...] = (up_b * scale).astype(HALF)
            first = first + jnp.sum(hid * unit_raw, axis=1, keepdims=True)
            second = second + jnp.sum(gate_b * gate_raw + up_b * up_raw, axis=1, keepdims=True)
        lanes = iota((tall, 128), 1)
        r.values[row, :] = jnp.where(lanes == 0, first, jnp.where(lanes == 1, second, 0.0))

    loop(total // tall, some_rows)
    r.value_src[...] = jnp.zeros_like(r.value_src)

    def fill_value(j):
        r.value_src[j, :, :cap] = exact(eye8, r.values[strip(j), :], NT)

    loop(blocks, fill_value)
    value_start()
    r.value_all[block] = r.value_src[block]

    def input_term(d):
        result = None
        for back, weight in zip(gu_back, gu_w):
            term = fast(back[...], weight[columns(d), :], NT)
            result = term if result is None else result + term
        return result

    def output_term(d):
        return fast(r.hidden[...], down_w[:, columns(d)])

    tiles(1, input_term)

    value_arrive()

    def add_values(j, kept):
        return kept + exact(r.value_all[j, :, :cap], r.table[strip(j), :])

    inner_part = lax.fori_loop(0, blocks, add_values, jnp.zeros((8, 2 * count), FULL))
    inner_launch(inner_part)

    tiles(0, output_term)

    wide_cut = 256

    def weight_grads(lo, hi):
        def one(i):
            at = pl.ds(pl.multiple_of(i * wide_cut, wide_cut), wide_cut)
            if fused:
                value = fast(rows[:, at], gu_back2[0][...], TN)
                r.gate_grad[at, :] = value[:, :units].astype(HALF)
                r.up_grad[at, :] = value[:, units:].astype(HALF)
            else:
                r.gate_grad[at, :] = fast(rows[:, at], gu_back2[0][...], TN).astype(HALF)
                r.up_grad[at, :] = fast(rows[:, at], gu_back2[1][...], TN).astype(HALF)

        lax.fori_loop(lo, hi, lambda i, c: (one(i), c)[1], 0)

    def down_grads(lo, hi):
        for at, span in slices(units, 256)[lo:hi]:
            r.down_grad[at : at + span, :] = fast(
                r.hidden2[:, at : at + span], grads[...], TN
            ).astype(HALF)

    cuts = features // wide_cut
    down_cuts = len(slices(units, 256))
    weight_grads(0, cuts // 2)

    inner_arrive()
    inner_all = jnp.sum(r.inner_all[...], axis=0)
    gap_grad = first_weight * second_weight * (inner_all[0:1, :count] - inner_all[0:1, count:])
    inner_row = inner_all[1:2, :count] + inner_all[1:2, count:] + gap_grad * raw_gap
    row8 = iota((8, count), 0)
    packed = jnp.where(row8 == 0, scale_row, 0.0)
    packed = jnp.where(row8 == 1, inner_row, packed)
    packed = jnp.where(row8 == 2, gap_grad, packed)
    packed = jnp.where(row8 == 3, first_weight, packed)
    packed = jnp.where(row8 == 4, second_weight, packed)
    packed_cols = to_columns(packed)
    scale_two, inner_col = (packed_cols[:, 0:1], packed_cols[:, 1:2])
    gap_col = packed_cols[:, 2:3]
    weight_one, weight_two = (packed_cols[:, 3:4], packed_cols[:, 4:5])
    resid_f = r.resid[...].astype(FULL)
    router_launch(exact(gap_grad * hot_gap_row, resid_f * scale_two))
    upstream = r.out_grad[...].astype(FULL)
    r.base[...] = (
        upstream
        + scale_two * exact(gap_col * (first_col - second_col), router)
        - resid_f * (scale_two * scale_two * scale_two) * (inner_col / features)
    )

    finish(1)
    weight_grads(cuts // 2, cuts)
    backs_arrive(1)
    moe_grad = fast(r.across[:count, :], backs[1][...])
    moe_grad = moe_grad + fast(r.across[count:, :], backs[1][...])
    resid_grad = r.base[...] + scale_two * moe_grad
    r.resid_grad[...] = resid_grad
    sgrad_launch(exact(c_side, grow_wide * resid_grad))
    finish(0)

    normed = r.normed[...]
    pairing_back = exact(b_side, c_side, TN)
    upper = iota((count, count), 0) <= iota((count, count), 1)
    step_wide = spread_heads(step_col)
    lane8 = iota((8, 128), 1)
    row128 = iota((8, 128), 0)
    rate_parts = jnp.zeros((1, 128), FULL)
    for h in range(heads):
        at = slice(h * count, (h + 1) * count)
        own = jnp.where(lane_head == h, resid_grad, 0.0)
        pull = exact(own, normed, NT) * r.mixing[:, at]
        gap = sum_col[:, h : h + 1] - sum_row[h : h + 1, :]
        found = jnp.sum(jnp.sum(pull * gap, axis=0, keepdims=True), axis=1, keepdims=True)
        rate_parts = jnp.where(lane8[0:1] == h, found, rate_parts)
        r.stack[at, :] = own
    for h in range(heads):
        at = slice(h * count, (h + 1) * count)
        rise = -(run_col[:, h : h + 1] + sum_row[h : h + 1, :] * rate[0:1, h : h + 1])
        table = jnp.where(upper, jnp.exp(jnp.where(upper, rise, 0.0)), 0.0)
        r.mixing[:, at] = table * pairing_back
    local_grad = step_wide * exact(r.mixing[...], r.stack[...]) + skip_wide * resid_grad
    skip_lanes = jnp.sum(resid_grad * normed, axis=0, keepdims=True)
    rate_lanes = jnp.sum(resid_grad * r.carried[...] * sum_wide, axis=0, keepdims=True)
    down_grads(0, down_cuts // 2)

    sgrad_arrive()
    state_grad = carry(r.sgrad_all, True)
    tail_grad = tail_wide * exact(b_side, state_grad, TN)
    normed_grad = local_grad + tail_grad
    last_launch(exact(ones_row, normed_grad * inputs, NT))
    sum_end = sum_wide[count - 1 : count, :]
    rate_lanes = rate_lanes + jnp.sum(
        normed * tail_grad * (sum_end - sum_wide), axis=0, keepdims=True
    )
    rate_lanes = rate_lanes + sum_end * decay_wide * jnp.sum(
        state_grad * state_in, axis=0, keepdims=True
    )
    head_hot = (iota((width, 128), 0) // head_dim == iota((width, 128), 1)).astype(FULL)
    row_wide = iota((8, width), 0)
    lanes = jnp.where(row_wide == 0, rate_lanes, jnp.where(row_wide == 1, skip_lanes, 0.0))
    small_part = exact(lanes, head_hot)
    small_part = jnp.where(row128 == 0, -(small_part + rate_parts), small_part)
    small_launch(small_part)

    down_grads(down_cuts // 2, down_cuts)
    backs_arrive(0)
    first_out = fast(r.across[:count, :], backs[0][...])
    second_out = fast(r.across[count:, :], backs[0][...])
    r.block_out[...] = (resid_f + (weight_one * first_out + weight_two * second_out)).astype(HALF)
    router_arrive()
    router_total = jnp.sum(r.rout_all[...], axis=0)
    r.router_grad[...] = router_total[1 : 1 + experts]

    last_arrive()
    inner_one = to_columns(jnp.sum(r.last_all[...], axis=0))[:, 0:1]
    r.token_grad[...] = (
        resid_grad
        + scale_one * normed_grad
        - inputs * (scale_one * scale_one * scale_one) * (inner_one / features)
    ).astype(HALF)
    small_arrive()
    r.small[...] = jnp.sum(r.small_all[...], axis=0)

    for sent in (
        square_sent,
        decay_sent,
        state_sent,
        stat_sent,
        inner_sent,
        sgrad_sent,
        router_sent,
        last_sent,
        small_sent,
        slot_sent,
        value_sent,
    ):
        sent()
    for t in range(2):

        def sent_back(n):
            back_copy(t, n + 1, block).wait_send()
            z_copy(t, n + 1, block).wait_send()

        loop(blocks - 1, sent_back)
        loop(chip_count, lambda c: pair_copy(t, c).wait_send())
        loop(chip_count - 1, lambda q: chip_copy(t, q + 1).wait_send())

        def spread_done(n):
            k, q = (n // (chip_count - 1), lax.rem(n, chip_count - 1) + 1)
            spread_copy(t, k, origin_of(k), q, place).wait_send()

        loop(blocks * (chip_count - 1), spread_done)

        def partner_done(n):
            k, q = (n // chip_count, lax.rem(n, chip_count))
            partner_copy(t, k, origin_of(k), q, place).wait_send()

        loop(blocks * chip_count, partner_done)


def body(
    tokens,
    routes,
    dt_raw,
    b_proj,
    c_proj,
    decay_rate,
    skip_gain,
    router_weight,
    gate_weight,
    up_weight,
    down_weight,
    out_grad,
):
    peers, blocks = (lax.axis_size(DP), lax.axis_size(EXPERT))
    chip_count = peers // 2
    count, width = tokens.shape
    features, units = gate_weight.shape[1:]
    experts, heads, state = (router_weight.shape[1], decay_rate.shape[0], b_proj.shape[1])
    capacity = 5 * count // (2 * blocks)
    cap = -(-capacity // 16) * 16
    total = blocks * cap
    fused = units % 128 == 0
    stat_rows = -(-(1 + experts) // 8) * 8
    vmem = pl.BlockSpec(memory_space=pltpu.VMEM)
    hbm = pl.BlockSpec(memory_space=pl.ANY)
    dma = pltpu.SemaphoreType.DMA
    given = dict(
        tokens=(tokens, vmem),
        routes=(routes.T, vmem),
        dt=(dt_raw.T, vmem),
        b_proj=(b_proj.T, vmem),
        c_proj=(c_proj.T, vmem),
        rate=(decay_rate[None], vmem),
        skip=(skip_gain[None], vmem),
        router=(router_weight.T, vmem),
        gate_hbm=(gate_weight, hbm),
        up_hbm=(up_weight, hbm),
        down_hbm=(down_weight, hbm),
        out_grad=(out_grad, vmem),
    )
    made = dict(
        block_out=((count, width), HALF),
        token_grad=((count, width), HALF),
        gate_grad=((features, units), HALF),
        up_grad=((features, units), HALF),
        down_grad=((units, features), HALF),
        router_grad=((experts, width), FULL),
        small=((8, 128), FULL),
    )
    if fused:
        split = dict(
            gu_w=((features, 2 * units), HALF),
            gu_s=((total, 2 * units), FULL),
            gu_back=((total, 2 * units), HALF),
            gu_back2=((total, 2 * units), HALF),
        )
    else:
        split = dict(
            gate_w=((features, units), HALF),
            gate_s=((total, units), FULL),
            gate_back=((total, units), HALF),
            gate_back2=((total, units), HALF),
            up_w=((features, units), HALF),
            up_s=((total, units), FULL),
            up_back=((total, units), HALF),
            up_back2=((total, units), HALF),
        )
    scratch = dict(
        split,
        down_w=((units, features), HALF),
        rows=((total, features), HALF),
        grads=((total, features), HALF),
        send_rows=((total, width), HALF),
        send_grads=((total, width), HALF),
        back_f=((total, width), HALF),
        back_b=((total, width), HALF),
        unit_raw=((total, units), FULL),
        hidden=((total, units), HALF),
        hidden2=((total, units), HALF),
        away=((2, chip_count, total, width), HALF),
        mine=((2, chip_count, total, width), HALF),
        pair=((2, chip_count, total, width), HALF),
        chips=((2, chip_count, total, width), HALF),
        summed=((2, total, width), HALF),
        table=((total, 2 * count), FULL),
        across=((2 * count, total), HALF),
        normed=((count, width), FULL),
        local=((count, width), FULL),
        carried=((count, width), FULL),
        base=((count, width), FULL),
        resid_grad=((count, width), FULL),
        resid=((count, width), HALF),
        mixing=((count, heads * count), FULL),
        stack=((heads * count, width), FULL),
        slot_weight=((total, 128), FULL),
        slot_scale=((total, 128), FULL),
        values=((total, 128), FULL),
        slot_src=((blocks, 8, 128), FULL),
        slot_all=((blocks, 8, 128), FULL),
        value_src=((blocks, 8, 128), FULL),
        value_all=((blocks, 8, 128), FULL),
    )
    exchanged = dict(
        square=(DP, (8, count)),
        decay=(EXPERT, (8, width)),
        state=(EXPERT, (state, width)),
        stat=(DP, (stat_rows, count)),
        inner=(DP, (8, 2 * count)),
        sgrad=(EXPERT, (state, width)),
        rout=(EXPERT, (stat_rows, width)),
        last=(DP, (8, count)),
        small=(EXPERT, (8, 128)),
    )
    counts = dict(slot=blocks, value=blocks)
    for name, (axis, shape) in exchanged.items():
        counts[name] = lax.axis_size(axis)
        scratch[name + SRC] = (shape, FULL)
        scratch[name + ALL] = ((counts[name],) + shape, FULL)
    shapes = {name: (amount,) for name, amount in counts.items()}
    shapes.update(
        z=(2, blocks),
        c=(2, blocks * chip_count),
        p=(2, blocks * chip_count),
        pair=(2, chip_count),
        chip=(2, chip_count),
        back=(2, blocks),
    )
    sems = {name + way: dma(shape) for name, shape in shapes.items() for way in (SEND, RECV)}
    sems.update(local_sem=dma((2,)), weight_sem=dma((3,)))
    names = [*given, *made, *scratch, *sems]
    block_out, token_grad, gate_part, up_part, down_part, router_part, small = pl.pallas_call(
        functools.partial(step_kernel, names, capacity, cap, fused),
        out_shape=[jax.ShapeDtypeStruct(shape, kind) for shape, kind in made.values()],
        in_specs=[spec for _, spec in given.values()],
        out_specs=[vmem] * len(made),
        scratch_shapes=[pltpu.VMEM(shape, kind) for shape, kind in scratch.values()]
        + list(sems.values()),
        compiler_params=pltpu.CompilerParams(
            collective_id=7, has_side_effects=True, vmem_limit_bytes=40 << 20
        ),
        name="step",
    )(*[array for array, _ in given.values()])
    return (
        block_out,
        token_grad,
        gate_part[None],
        up_part[None],
        down_part[None],
        router_part.T,
        small[0, :heads],
        small[1, :heads],
    )


def solution(mesh):
    return jax.shard_map(
        body,
        mesh=mesh,
        in_specs=(
            P(EXPERT, DP),
            P(EXPERT, None),
            P(EXPERT, DP),
            P(EXPERT, None),
            P(EXPERT, None),
            P(DP),
            P(DP),
            P(DP, None),
            P(EXPERT, None, DP),
            P(EXPERT, None, DP),
            P(EXPERT, DP, None),
            P(EXPERT, DP),
        ),
        out_specs=(
            P(EXPERT, DP),
            P(EXPERT, DP),
            P(EXPERT, None, DP),
            P(EXPERT, None, DP),
            P(EXPERT, DP, None),
            P(DP, None),
            P(DP),
            P(DP),
        ),
        check_vma=False,
    )
```

time: 140 us -> 84.5 us (0.60)
  matrix products: 26.9 us -> 0 us
  Pallas kernels: 90.3 us -> 69.1 us
  other arithmetic: 10 us -> 0 us
  local copies, waits for them, and re-layouts: 10.6 us -> 14.3 us
    dot_general x24 -> x0, matrix products: 26.9 us -> none  [the longest x1 4.12 us: body(): lax.dot_general(unit_rows, up_back, tn, preferred_element_type=jnp.float32)]
    pallas_call x7 -> x1, Pallas kernels: 90.3 us -> 69.1 us  [body(): pl.pallas_call(functools.partial(step_kernel, names, capacity, cap, fused...]
    unnamed x33 -> x24, local copies, waits for them, and re-layouts: 4.05 us -> 13.8 us
    reduce_sum x8 -> x0, other arithmetic: 2.82 us -> none  [the longest x1 0.99 us: ssd_piece(): state_end = decay_total[:, None] * state_start + local_state]
    slice x4 -> x0, local copies, waits for them, and re-layouts: 2.64 us -> none  [the longest x3 2.39 us: carry_in(): held = jnp.where(reached, decays[at][:, None] * held + states[at], held)]
    squeeze x9 -> x1, local copies, waits for them, and re-layouts: 2.01 us -> 0.52 us  [body(): small[1, :heads]]
    mul x5 -> x0, other arithmetic: 1.48 us -> none  [the longest x1 0.69 us: body(): scale_one * scale_one * scale_one]
where the time goes in v1:
time: 84.5 us; the launch traced here: 84.1 us
  Pallas kernels  69.1 us (82%)
  local copies, waits for them, and re-layouts  14.3 us (17%)
    pallas_call x1, Pallas kernels, body(): pl.pallas_call(functools.partial(step_kernel, names, capacity, cap, fused...  69.1 us
    unnamed x24, local copies, waits for them, and re-layouts  13.8 us

profile of v1, /device:TPU:0, one launch (start us, length us, event | category | flops | bytes accessed | tf_op | source)
XLA Modules:
  0.0 84.1 jit_solution(7136654654187775931)
XLA Ops:
  0.6 0.0 copy-start
  0.6 0.8 copy-done
  1.5 0.0 copy-start.1
  1.5 0.8 copy-done.1
  2.3 0.0 copy-start.2
  2.3 0.7 copy-done.2
  3.0 0.0 copy-start.3
  3.0 0.7 copy-done.3
  3.7 0.0 copy-start.4
  3.7 0.7 copy-done.4
  4.4 0.0 copy-start.5
  4.4 0.7 copy-done.5
  5.1 0.0 copy-start.6
  5.1 0.7 copy-done.6
  5.8 0.0 copy-start.7
  5.8 0.7 copy-done.7
  6.4 0.0 copy-start.8
  6.4 0.7 copy-done.8
  7.1 69.1 %step.1 = (bf16[128,256]{1,0:T(8,128)(2,1)S(1)}, bf16[128,256]{1,0:T(8,128)(2,1)S(1)}, bf16[2048,896]{1,0:T(8,128)(2,1)S(1)}, bf16[2048,896]{1,0:T(8,128)(2,1)S(...) custom-call(bf16[128,256]{1,0:T(8,128)(2,1)S(1)} %copy-done, ...), custom_call_target="tpu_custom_call" | custom-call | tf_op jit(solution)/shard_map/step/pallas_call | solution.py:853
  76.2 0.5 slice_bitcast_fusion
  76.7 0.6 copy.26
  77.3 0.6 copy.27
  78.0 1.8 %copy.28 = bf16[1,2048,896]{2,1,0:T(8,128)(2,1)} copy(bf16[1,2048,896]{2,1,0:T(8,128)(2,1)S(1)} %bitcast.17) | data formatting | bytes 7340032
  79.8 1.8 %copy.29 = bf16[1,2048,896]{2,1,0:T(8,128)(2,1)} copy(bf16[1,2048,896]{2,1,0:T(8,128)(2,1)S(1)} %bitcast.16) | data formatting | bytes 7340032
  81.6 1.8 %copy.30 = bf16[1,896,2048]{2,1,0:T(8,128)(2,1)} copy(bf16[1,896,2048]{2,1,0:T(8,128)(2,1)S(1)} %bitcast.15) | data formatting | bytes 7340032
  83.5 0.6 copy.31
Async XLA Ops:
  0.6 0.8 copy-start
  1.5 0.8 copy-start.1
  2.3 0.7 copy-start.2
  3.0 0.7 copy-start.3
  3.7 0.7 copy-start.4
  4.4 0.7 copy-start.5
  5.1 0.7 copy-start.6
  5.8 0.7 copy-start.7
  6.4 0.7 copy-start.8

commit v2 on v1

--- a/solution.py
+++ b/solution.py
@@ -12,7 +12,7 @@
 HIGHEST = lax.Precision.HIGHEST
 MESH = pl.DeviceIdType.MESH
 DP, EXPERT = ("dp", "expert")
-SEND, RECV, SRC, ALL = ("_send", "_recv", "_src", "_all")
+SEND, RECV, SRC, ALL, SEMS, HBM = ("_send", "_recv", "_src", "_all", "_sems", "_hbm")
 HALF, FULL = (jnp.bfloat16, jnp.float32)
 NN = (((1,), (0,)), ((), ()))
 NT = (((1,), (1,)), ((), ()))
@@ -48,10 +48,10 @@
 
 
 def sigmoid(v):
-    return 1.0 / (1.0 + jnp.exp(-v))
-
-
-def step_kernel(names, capacity, cap, fused, *refs):
+    return 0.5 + 0.5 * jnp.tanh(0.5 * v)
+
+
+def step_kernel(names, loaded, capacity, cap, fused, *refs):
     r = types.SimpleNamespace(**dict(zip(names, refs)))
     peers, place = (lax.axis_size(DP), lax.axis_index(DP))
     blocks, block = (lax.axis_size(EXPERT), lax.axis_index(EXPERT))
@@ -85,11 +85,32 @@
     def origin_of(k):
         return lax.rem(block + blocks - k, blocks)
 
-    def chip_at(q):
-        return lax.rem(chip + q, chip_count)
-
-    def chip_from(q):
-        return lax.rem(chip + chip_count - q, chip_count)
+    square = chip_count == 4
+
+    def turn(along_u, along_v):
+        along_x = (1 - core) * along_u + core * along_v
+        along_y = core * along_u + (1 - core) * along_v
+        x = lax.rem(lax.rem(chip, 2) + along_x, 2)
+        return 2 * lax.rem(chip // 2 + along_y, 2) + x
+
+    def chip_to(way):
+        if square:
+            return turn((1, 0, 1)[way], (0, 1, 1)[way])
+        return lax.rem(chip + way + 1, chip_count)
+
+    def chip_from(way):
+        return chip_to(way) if square else lax.rem(chip + chip_count - way - 1, chip_count)
+
+    def partner_chip(way):
+        if way < 0:
+            return chip
+        return chip_to((1, 0, 2)[way]) if square else chip_from(way)
+
+    def chip_in_turn(q):
+        if square:
+            x = lax.rem(lax.rem(chip, 2) + 1 - q // 2, 2)
+            return 2 * lax.rem(chip // 2 + 1 - lax.rem(q, 2), 2) + x
+        return lax.rem(chip + q + 1, chip_count)
 
     if fused:
         gu_w, gu_s = ((r.gu_w,), (r.gu_s,))
@@ -114,7 +135,11 @@
             ((r.down_hbm, down_w), (r.gate_hbm, halves[0]), (r.up_hbm, halves[1]))
         )
     ]
-    for item in weights:
+    loads = {
+        name: pltpu.make_async_copy(getattr(r, name + HBM), getattr(r, name), r.load_sem.at[n])
+        for n, name in enumerate(loaded)
+    }
+    for item in loads.values():
         item.start()
 
     barrier = pltpu.get_barrier_semaphore()
@@ -127,39 +152,37 @@
 
         loop(amount - 1, signal)
 
-    def exchange(axis, src, land, sems):
+    def waits(ref, sems):
+        whole = pltpu.make_async_remote_copy(
+            src_ref=ref,
+            dst_ref=ref,
+            send_sem=sems[0],
+            recv_sem=sems[1],
+            device_id={DP: partner},
+            device_id_type=MESH,
+        )
+        return whole.wait_recv, whole.wait_send
+
+    def exchange(axis, src, everyone, sems):
         amount, me = (peers, place) if axis == DP else (blocks, block)
-        send, recv = (getattr(r, sems + SEND), getattr(r, sems + RECV))
-
-        def copy(k, at):
-            return pltpu.make_async_remote_copy(
-                src_ref=src(lax.rem(me + k, amount)),
-                dst_ref=land(at),
-                send_sem=send.at[k],
-                recv_sem=recv.at[k],
-                device_id={axis: lax.rem(me + k, amount)},
+
+        def one(k):
+            to = lax.rem(me + k + 1, amount)
+            pltpu.make_async_remote_copy(
+                src_ref=src(to),
+                dst_ref=everyone.at[me],
+                send_sem=sems.at[0],
+                recv_sem=sems.at[1],
+                device_id={axis: to},
                 device_id_type=MESH,
-            )
-
-        def start():
-            loop(amount - 1, lambda k: copy(k + 1, me).start())
-
-        def arrive():
-            loop(
-                amount - 1,
-                lambda k: copy(k + 1, lax.rem(me + amount - k - 1, amount)).wait_recv(),
-            )
-
-        def sent():
-            loop(amount - 1, lambda k: copy(k + 1, me).wait_send())
-
-        return start, arrive, sent
+            ).start()
+
+        arrive, sent = waits(everyone.at[: amount - 1], (sems.at[0], sems.at[1]))
+        return lambda: loop(amount - 1, one), arrive, sent
 
     def shared(axis, name):
         src, everyone = (getattr(r, name + SRC), getattr(r, name + ALL))
-        start, arrive, sent = exchange(
-            axis, lambda _: src, lambda at: everyone.at[at], name
-        )
+        start, arrive, sent = exchange(axis, lambda _: src, everyone, getattr(r, name + SEMS))
 
         def launch(value):
             src[...] = value
@@ -178,10 +201,10 @@
     last_launch, last_arrive, last_sent = shared(DP, "last")
     small_launch, small_arrive, small_sent = shared(EXPERT, "small")
     slot_start, slot_arrive, slot_sent = exchange(
-        EXPERT, lambda to: r.slot_src.at[to], lambda at: r.slot_all.at[at], "slot"
+        EXPERT, lambda to: r.slot_src.at[to], r.slot_all, r.slot_sems
     )
     value_start, value_arrive, value_sent = exchange(
-        EXPERT, lambda to: r.value_src.at[to], lambda at: r.value_all.at[at], "value"
+        EXPERT, lambda to: r.value_src.at[to], r.value_all, r.value_sems
     )
 
     def own_copy(t):
@@ -195,30 +218,30 @@
         return pltpu.make_async_remote_copy(
             src_ref=sources[t].at[strip(ahead(k)), :],
             dst_ref=wholes[t].at[strip(land), columns(place)],
-            send_sem=r.z_send.at[t, k],
-            recv_sem=r.z_recv.at[t, k],
+            send_sem=r.z_send.at[t],
+            recv_sem=r.z_recv.at[t, k - 1],
             device_id={EXPERT: ahead(k)},
             device_id_type=MESH,
         )
 
-    def spread_copy(t, k, j, q, owner):
-        cut = wholes[t].at[strip(j), columns(owner)]
+    def spread_copy(t, k, way, owner, to):
+        cut = wholes[t].at[strip(origin_of(k)), columns(owner)]
         return pltpu.make_async_remote_copy(
             src_ref=cut,
             dst_ref=cut,
-            send_sem=r.c_send.at[t, k * chip_count + q],
-            recv_sem=r.c_recv.at[t, k * chip_count + q],
-            device_id={DP: 2 * chip_at(q) + core},
+            send_sem=r.c_send.at[t],
+            recv_sem=r.c_recv.at[t, way, k],
+            device_id={DP: 2 * to + core},
             device_id_type=MESH,
         )
 
-    def partner_copy(t, k, j, q, owner):
-        cut = wholes[t].at[strip(j), columns(owner)]
+    def partner_copy(t, way, owner):
+        cut = wholes[t].at[:, columns(owner)]
         return pltpu.make_async_remote_copy(
             src_ref=cut,
             dst_ref=cut,
-            send_sem=r.p_send.at[t, k * chip_count + q],
-            recv_sem=r.p_recv.at[t, k * chip_count + q],
+            send_sem=r.p_send.at[t],
+            recv_sem=r.p_recv.at[t, way + 1],
             device_id={DP: partner},
             device_id_type=MESH,
         )
@@ -227,53 +250,53 @@
         own_copy(t).start()
         loop(blocks - 1, lambda k: z_copy(t, k + 1, block).start())
 
-    def forward(t, k, j):
-        loop(chip_count - 1, lambda q: spread_copy(t, k, j, q + 1, place).start())
-        partner_copy(t, k, j, 0, place).start()
+    def forward(t, k):
+        for way in range(2 if square and t == 0 else chip_count - 1):
+            spread_copy(t, k, way, place, chip_to(way)).start()
 
     def forward_own(t):
         own_copy(t).wait()
-        forward(t, 0, block)
+        forward(t, 0)
 
     def pass_on(t):
         def one(n):
             z_copy(t, n + 1, origin_of(n + 1)).wait_recv()
-            forward(t, n + 1, origin_of(n + 1))
+            forward(t, n + 1)
 
         loop(blocks - 1, one)
-
-    def from_chip(t, q):
-        owner = 2 * chip_from(q) + core
+        partner_copy(t, -1, place).start()
+
+    def from_chip(t, way):
+        owner = 2 * chip_from(way) + core
 
         def one(k):
-            spread_copy(t, k, origin_of(k), q, owner).wait_recv()
-            partner_copy(t, k, origin_of(k), q, owner).start()
+            spread_copy(t, k, way, owner, chip_to(way)).wait_recv()
+            if square and t == 0 and way == 0:
+                spread_copy(t, k, 2, owner, chip_to(1)).start()
 
         loop(blocks, one)
-
-    def from_partner(t, q):
-        owner = 2 * chip_from(q) + 1 - core
-        loop(
-            blocks, lambda k: partner_copy(t, k, origin_of(k), q, owner).wait_recv()
-        )
+        partner_copy(t, way, owner).start()
+
+    def from_partner(t, way):
+        partner_copy(t, way, 2 * partner_chip(way) + 1 - core).wait_recv()
 
     def pair_copy(t, c):
         return pltpu.make_async_remote_copy(
             src_ref=away.at[t, c],
             dst_ref=pair.at[t, c],
-            send_sem=r.pair_send.at[t, c],
+            send_sem=r.pair_send.at[t],
             recv_sem=r.pair_recv.at[t, c],
             device_id={DP: partner},
             device_id_type=MESH,
         )
 
-    def chip_copy(t, q):
+    def chip_copy(t, way, c, to):
         return pltpu.make_async_remote_copy(
-            src_ref=mine.at[t, chip_at(q)],
-            dst_ref=chips.at[t, q],
-            send_sem=r.chip_send.at[t, q],
-            recv_sem=r.chip_recv.at[t, q],
-            device_id={DP: 2 * chip_at(q) + core},
+            src_ref=mine.at[t, c],
+            dst_ref=chips.at[t, way],
+            send_sem=r.chip_send.at[t],
+            recv_sem=r.chip_recv.at[t, way],
+            device_id={DP: 2 * to + core},
             device_id_type=MESH,
         )
 
@@ -281,47 +304,69 @@
         return pltpu.make_async_remote_copy(
             src_ref=summed.at[t, strip(ahead(k)), :],
             dst_ref=backs[t].at[strip(land), :],
-            send_sem=r.back_send.at[t, k],
-            recv_sem=r.back_recv.at[t, k],
+            send_sem=r.back_send.at[t],
+            recv_sem=r.back_recv.at[t],
             device_id={EXPERT: ahead(k)},
             device_id_type=MESH,
         )
 
-    def tiles(t, term):
+    def tiles(t, term, between=None):
+        def settle(c):
+            pair_copy(t, c).wait_recv()
+            mine[t, c] = (r.held[...] + pair[t, c].astype(FULL)).astype(HALF)
+
         def step(q):
-            @pl.when(q < chip_count)
-            def _():
-                c = chip_at(lax.rem(q + 1, chip_count))
-                away[t, c] = term(2 * c + 1 - core).astype(HALF)
-                pair_copy(t, c).start()
+            if between is not None:
+                pl.when(q == 2)(between)
+            value = term(chip_in_turn(q))
+            left, right = (value[:, :width], value[:, width:])
+            away[t, chip_in_turn(q)] = jnp.where(core == 0, right, left).astype(HALF)
+            pair_copy(t, chip_in_turn(q)).start()
 
             @pl.when(q > 0)
             def _():
-                c = chip_at(lax.rem(q, chip_count))
-                value = term(2 * c + core)
-                pair_copy(t, c).wait_recv()
-                mine[t, c] = (value + pair[t, c].astype(FULL)).astype(HALF)
-
-                @pl.when(q < chip_count)
-                def _():
-                    chip_copy(t, q).start()
-
-        loop(chip_count + 1, step)
+                c = chip_in_turn(q - 1)
+                settle(c)
+                if square:
+                    for way, when in ((0, 1), (1, 2 + core)):
+
+                        @pl.when(q == when)
+                        def _():
+                            chip_copy(t, way, c, chip_to(0)).start()
+                else:
+                    chip_copy(t, q - 1, c, c).start()
+
+            r.held[...] = jnp.where(core == 0, left, right)
+
+        loop(chip_count, step)
+        settle(chip)
+
+    def combine(t):
+        if square:
+            c = chip_to(1)
+            chip_copy(t, 0, c, c).wait_recv()
+            mine[t, c] = (mine[t, c].astype(FULL) + chips[t, 0].astype(FULL)).astype(HALF)
+            chip_copy(t, 2, c, c).start()
 
     def finish(t):
         value = mine[t, chip].astype(FULL)
-        for q in range(1, chip_count):
-            chip_copy(t, q).wait_recv()
-            value = value + chips[t, q].astype(FULL)
+        for way in range(1 if square else 0, chip_count - 1):
+            chip_copy(t, way, chip, chip_to(way)).wait_recv()
+            value = value + chips[t, way].astype(FULL)
         summed[t] = value.astype(HALF)
         loop(blocks - 1, lambda k: back_copy(t, k + 1, block).start())
         backs[t][strip(block), :] = summed[t, strip(block), :]
 
     def backs_arrive(t):
-        loop(
-            blocks - 1, lambda n: back_copy(t, n + 1, origin_of(n + 1)).wait_recv()
-        )
-
+        arrive, _ = waits(
+            backs[t].at[: (blocks - 1) * cap], (r.back_send.at[t], r.back_recv.at[t])
+        )
+        arrive()
+
+    for item in loads.values():
+        item.wait()
+    for item in weights:
+        item.start()
     inputs = r.tokens[...].astype(FULL)
     lane_head = iota((1, width), 1) // head_dim
 
@@ -408,8 +453,8 @@
         r.mixing[:, h * count : (h + 1) * count] = table * pairing * step_row[h : h + 1, :]
         r.stack[h * count : (h + 1) * count, :] = jnp.where(lane_head == h, normed, 0.0)
     r.local[...] = exact(r.mixing[...], r.stack[...]) + skip_wide * normed
+
     pass_on(1)
-
     decay_arrive()
     state_arrive()
 
@@ -436,8 +481,9 @@
     stat_part = exact(router_row, resid_f, NT)
     stat_launch(jnp.where(iota((stat_rows, count), 0) == 0, squares, stat_part))
     forward_own(0)
-    for q in range(1, chip_count):
-        from_chip(1, q)
+    pass_on(0)
+    for way in range(chip_count - 1):
+        from_chip(1, way)
 
     stat_arrive()
     stats = jnp.sum(r.stat_all[...], axis=0)
@@ -446,34 +492,19 @@
     first_weight = sigmoid(raw_gap * scale_row)
     second_weight = sigmoid(-raw_gap * scale_row)
     pick8 = iota((8, 2 * count), 0)
-    slot_rows = jnp.where(pick8 == 0, jnp.concatenate([first_weight, second_weight], axis=1), 0.0)
-    slot_rows = jnp.where(pick8 == 1, jnp.concatenate([scale_row, scale_row], axis=1), slot_rows)
+    slot_rows = jnp.zeros((8, 2 * count), FULL)
+    for n, both in enumerate(((first_weight, second_weight), (scale_row, scale_row))):
+        value = jnp.concatenate(both, axis=1)
+        near = value.astype(HALF).astype(FULL)
+        slot_rows = jnp.where(pick8 == 2 * n, near, slot_rows)
+        slot_rows = jnp.where(pick8 == 2 * n + 1, value - near, slot_rows)
     r.slot_src[...] = jnp.zeros_like(r.slot_src)
 
-    def fill_slot(e):
-        r.slot_src[e, :, :cap] = exact(slot_rows, r.table[strip(e), :], NT)
-
-    loop(blocks, fill_slot)
+    slot_wide = fast(slot_rows.astype(HALF), r.table[...].astype(HALF), NT)
+    for e in range(blocks):
+        r.slot_src[e, :, :cap] = slot_wide[:, e * cap : (e + 1) * cap]
     slot_start()
     r.slot_all[block] = r.slot_src[block]
-    pass_on(0)
-
-    for q in range(chip_count):
-        from_partner(1, q)
-    weights[0].wait()
-    for at, span in slices(units, 256):
-        r.unit_raw[:, at : at + span] = fast(grads[...], down_w[at : at + span, :], NT)
-
-    slot_arrive()
-    pick = (iota((8, 256), 0) == iota((8, 256), 1) // 128).astype(FULL)
-
-    def take_slots(j):
-        wide = exact(r.slot_all[j], pick, TN)
-        r.slot_weight[strip(j), :] = wide[:cap, :128]
-        r.slot_scale[strip(j), :] = wide[:cap, 128:]
-
-    loop(blocks, take_slots)
-
     weights[1].wait()
     weights[2].wait()
     for held in gu_s:
@@ -483,80 +514,109 @@
         for held, weight in zip(gu_s, gu_w):
             held[...] += fast(rows[:, columns(d)], weight[columns(d), :])
 
-    def same_core(q):
-        @pl.when(q > 0)
-        def _():
-            from_chip(0, q)
-
-        chunk(2 * chip_from(q) + core)
-
-    loop(chip_count, same_core)
-
-    def other_core(q):
-        from_partner(0, q)
-        chunk(2 * chip_from(q) + 1 - core)
-
-    loop(chip_count, other_core)
+    chunk(place)
+    from_chip(0, 0)
+    for way in range(-1, chip_count - 1):
+        from_partner(1, way)
+    weights[0].wait()
+    for at, span in slices(units, 256):
+        r.unit_raw[:, at : at + span] = fast(grads[...], down_w[at : at + span, :], NT)
+
+    slot_arrive()
+    pick = (iota((8, 256), 0) // 2 == iota((8, 256), 1) // 128).astype(HALF)
+
+    wides = [fast(r.slot_all[j].astype(HALF), pick, TN) for j in range(blocks)]
+    for j, wide in enumerate(wides):
+        r.slot_weight[j * cap : (j + 1) * cap, :] = wide[:cap, :128]
+        r.slot_scale[j * cap : (j + 1) * cap, :] = wide[:cap, 128:]
+
+    for way in range(chip_count - 1):
+        if way > 0:
+            from_chip(0, way)
+        from_partner(0, way - 1)
+
+        def one(n):
+            other = 2 * partner_chip(way - 1) + 1 - core
+            chunk((1 - n) * other + n * (2 * chip_from(way) + core))
+
+        loop(2, one)
+    from_partner(0, chip_count - 2)
+    chunk(2 * partner_chip(chip_count - 2) + 1 - core)
 
     tall = 16
     r.values[...] = jnp.zeros_like(r.values)
+    span = 128 if units % 128 == 0 else 64
 
     def some_rows(i):
         row = pl.ds(pl.multiple_of(i * tall, tall), tall)
-        scale = r.slot_scale[row, 0:1]
-        weight = r.slot_weight[row, 0:1]
-        first = jnp.zeros((tall, 1), FULL)
-        second = jnp.zeros((tall, 1), FULL)
-        for at, span in slices(units, 256):
-            gate_raw = part(gu_s, 0, row, at, span)[...]
-            up_raw = part(gu_s, 1, row, at, span)[...]
-            unit_raw = r.unit_raw[row, at : at + span]
+        scale = r.slot_scale[row, :span]
+        weight = r.slot_weight[row, :span]
+        first = jnp.zeros((tall, span), FULL)
+        second = jnp.zeros((tall, span), FULL)
+        spans = range(0, units, span)
+        given = [
+            (
+                part(gu_s, 0, row, at, span)[...],
+                part(gu_s, 1, row, at, span)[...],
+                r.unit_raw[row, at : at + span],
+            )
+            for at in spans
+        ]
+        found = []
+        for gate_raw, up_raw, unit_raw in given:
             gate, up = (gate_raw * scale, up_raw * scale)
             sigma = sigmoid(gate)
             silu = gate * sigma
             hid = silu * up
             unit = unit_raw * weight
-            gate_b = unit * up * (sigma * (1.0 + gate * (1.0 - sigma)))
+            gate_b = unit * up * (sigma + silu * (1.0 - sigma))
             up_b = unit * silu
-            r.hidden[row, at : at + span] = hid.astype(HALF)
-            r.hidden2[row, at : at + span] = (hid * weight).astype(HALF)
-            part(gu_back, 0, row, at, span)[...] = gate_b.astype(HALF)
-            part(gu_back, 1, row, at, span)[...] = up_b.astype(HALF)
-            part(gu_back2, 0, row, at, span)[...] = (gate_b * scale).astype(HALF)
-            part(gu_back2, 1, row, at, span)[...] = (up_b * scale).astype(HALF)
-            first = first + jnp.sum(hid * unit_raw, axis=1, keepdims=True)
-            second = second + jnp.sum(gate_b * gate_raw + up_b * up_raw, axis=1, keepdims=True)
-        lanes = iota((tall, 128), 1)
-        r.values[row, :] = jnp.where(lanes == 0, first, jnp.where(lanes == 1, second, 0.0))
+            first = first + hid * unit_raw
+            second = second + (gate_b * gate_raw + up_b * up_raw)
+            values = (hid, hid * weight, gate_b, up_b, gate_b * scale, up_b * scale)
+            found.append([value.astype(HALF) for value in values])
+        for at, (hid, hid2, gate_b, up_b, gate_b2, up_b2) in zip(spans, found):
+            r.hidden[row, at : at + span] = hid
+            r.hidden2[row, at : at + span] = hid2
+            part(gu_back, 0, row, at, span)[...] = gate_b
+            part(gu_back, 1, row, at, span)[...] = up_b
+            part(gu_back2, 0, row, at, span)[...] = gate_b2
+            part(gu_back2, 1, row, at, span)[...] = up_b2
+        r.values[row, :span] = first
+        r.values[row, 128 : 128 + span] = second
 
     loop(total // tall, some_rows)
-    r.value_src[...] = jnp.zeros_like(r.value_src)
-
-    def fill_value(j):
-        r.value_src[j, :, :cap] = exact(eye8, r.values[strip(j), :], NT)
-
-    loop(blocks, fill_value)
-    value_start()
-    r.value_all[block] = r.value_src[block]
-
-    def input_term(d):
+    def send_values():
+        r.value_src[...] = jnp.zeros_like(r.value_src)
+        lane_sums = (iota((8, 256), 0) == iota((8, 256), 1) // 128).astype(FULL)
+        value_rows = exact(lane_sums, r.values[...], NT)
+        for j in range(blocks):
+            r.value_src[j, :, :cap] = value_rows[:, j * cap : (j + 1) * cap]
+        value_start()
+        r.value_all[block] = r.value_src[block]
+
+    def both_columns(c):
+        return pl.ds(pl.multiple_of(2 * c * width, 256), 2 * width)
+
+    def input_term(c):
         result = None
         for back, weight in zip(gu_back, gu_w):
-            term = fast(back[...], weight[columns(d), :], NT)
+            term = fast(back[...], weight[both_columns(c), :], NT)
             result = term if result is None else result + term
         return result
 
-    def output_term(d):
-        return fast(r.hidden[...], down_w[:, columns(d)])
-
-    tiles(1, input_term)
-
+    def output_term(c):
+        return fast(r.hidden[...], down_w[:, both_columns(c)])
+
+    tiles(1, input_term, send_values)
+
+    combine(1)
     value_arrive()
-
-    def add_values(j, kept):
-        return kept + exact(r.value_all[j, :, :cap], r.table[strip(j), :])
-
-    inner_part = lax.fori_loop(0, blocks, add_values, jnp.zeros((8, 2 * count), FULL))
+    inner_part = jnp.zeros((8, 2 * count), FULL)
+    for j in range(blocks):
+        inner_part = inner_part + exact(
+            r.value_all[j, :, :cap], r.table[j * cap : (j + 1) * cap, :]
+        )
     inner_launch(inner_part)
 
     tiles(0, output_term)
@@ -576,16 +636,11 @@
 
         lax.fori_loop(lo, hi, lambda i, c: (one(i), c)[1], 0)
 
-    def down_grads(lo, hi):
-        for at, span in slices(units, 256)[lo:hi]:
-            r.down_grad[at : at + span, :] = fast(
-                r.hidden2[:, at : at + span], grads[...], TN
-            ).astype(HALF)
-
     cuts = features // wide_cut
-    down_cuts = len(slices(units, 256))
+
+    finish(1)
     weight_grads(0, cuts // 2)
-
+    combine(0)
     inner_arrive()
     inner_all = jnp.sum(r.inner_all[...], axis=0)
     gap_grad = first_weight * second_weight * (inner_all[0:1, :count] - inner_all[0:1, count:])
@@ -609,16 +664,12 @@
         - resid_f * (scale_two * scale_two * scale_two) * (inner_col / features)
     )
 
-    finish(1)
-    weight_grads(cuts // 2, cuts)
     backs_arrive(1)
     moe_grad = fast(r.across[:count, :], backs[1][...])
     moe_grad = moe_grad + fast(r.across[count:, :], backs[1][...])
     resid_grad = r.base[...] + scale_two * moe_grad
     r.resid_grad[...] = resid_grad
     sgrad_launch(exact(c_side, grow_wide * resid_grad))
-    finish(0)
-
     normed = r.normed[...]
     pairing_back = exact(b_side, c_side, TN)
     upper = iota((count, count), 0) <= iota((count, count), 1)
@@ -642,7 +693,10 @@
     local_grad = step_wide * exact(r.mixing[...], r.stack[...]) + skip_wide * resid_grad
     skip_lanes = jnp.sum(resid_grad * normed, axis=0, keepdims=True)
     rate_lanes = jnp.sum(resid_grad * r.carried[...] * sum_wide, axis=0, keepdims=True)
-    down_grads(0, down_cuts // 2)
+    weight_grads(cuts // 2, 5 * cuts // 8)
+    finish(0)
+    weight_grads(5 * cuts // 8, cuts)
+
 
     sgrad_arrive()
     state_grad = carry(r.sgrad_all, True)
@@ -663,7 +717,6 @@
     small_part = jnp.where(row128 == 0, -(small_part + rate_parts), small_part)
     small_launch(small_part)
 
-    down_grads(down_cuts // 2, down_cuts)
     backs_arrive(0)
     first_out = fast(r.across[:count, :], backs[0][...])
     second_out = fast(r.across[count:, :], backs[0][...])
@@ -680,7 +733,9 @@
         - inputs * (scale_one * scale_one * scale_one) * (inner_one / features)
     ).astype(HALF)
     small_arrive()
-    r.small[...] = jnp.sum(r.small_all[...], axis=0)
+    small = jnp.sum(r.small_all[...], axis=0)
+    r.rate_grad[...] = small[0:1, :heads]
+    r.skip_grad[...] = small[1:2, :heads]
 
     for sent in (
         square_sent,
@@ -696,27 +751,42 @@
         value_sent,
     ):
         sent()
+    lead = (blocks - 1) * cap
     for t in range(2):
-
-        def sent_back(n):
-            back_copy(t, n + 1, block).wait_send()
-            z_copy(t, n + 1, block).wait_send()
-
-        loop(blocks - 1, sent_back)
-        loop(chip_count, lambda c: pair_copy(t, c).wait_send())
-        loop(chip_count - 1, lambda q: chip_copy(t, q + 1).wait_send())
-
-        def spread_done(n):
-            k, q = (n // (chip_count - 1), lax.rem(n, chip_count - 1) + 1)
-            spread_copy(t, k, origin_of(k), q, place).wait_send()
-
-        loop(blocks * (chip_count - 1), spread_done)
-
-        def partner_done(n):
-            k, q = (n // chip_count, lax.rem(n, chip_count))
-            partner_copy(t, k, origin_of(k), q, place).wait_send()
-
-        loop(blocks * chip_count, partner_done)
+        for ref, send, recv in (
+            (sources[t].at[:lead], r.z_send, r.z_recv.at[t, 0]),
+            (wholes[t].at[:, : (chip_count - 1) * width], r.c_send, r.c_recv.at[t, 0, 0]),
+            (wholes[t].at[:, : chip_count * width], r.p_send, r.p_recv.at[t, 0]),
+            (away.at[t], r.pair_send, r.pair_recv.at[t, 0]),
+            (mine.at[t, 1:], r.chip_send, r.chip_recv.at[t, 0]),
+            (summed.at[t, :lead], r.back_send, r.back_recv.at[t]),
+        ):
+            waits(ref, (send.at[t], recv))[1]()
+
+
+PIECES = 4
+
+
+def write_kernel(hidden, grads, *refs):
+    amount = (len(refs) - 2) // 2
+    ready, outs, down, sems = (refs[:amount], refs[amount:-2], refs[-2], refs[-1])
+    copies = []
+
+    def send(src, dst, rows, at):
+        cut = pl.ds(at, rows)
+        copies.append(pltpu.make_async_copy(src.at[cut], dst.at[cut], sems.at[len(copies)]))
+        copies[-1].start()
+
+    for src, dst in zip(ready, outs):
+        rows = src.shape[0]
+        pieces = PIECES if rows % (16 * PIECES) == 0 and rows >= 512 else 1
+        for at in range(0, rows, rows // pieces):
+            send(src, dst, rows // pieces, at)
+    for at, rows in slices(down.shape[0], 256):
+        down[at : at + rows, :] = fast(hidden[:, at : at + rows], grads[...], TN).astype(HALF)
+        send(down, outs[-1], rows, at)
+    for copy in copies:
+        copy.wait()
 
 
 def body(
@@ -744,30 +814,31 @@
     fused = units % 128 == 0
     stat_rows = -(-(1 + experts) // 8) * 8
     vmem = pl.BlockSpec(memory_space=pltpu.VMEM)
-    hbm = pl.BlockSpec(memory_space=pl.ANY)
+    hbm = pl.BlockSpec(memory_space=pltpu.HBM)
     dma = pltpu.SemaphoreType.DMA
-    given = dict(
-        tokens=(tokens, vmem),
-        routes=(routes.T, vmem),
-        dt=(dt_raw.T, vmem),
-        b_proj=(b_proj.T, vmem),
-        c_proj=(c_proj.T, vmem),
-        rate=(decay_rate[None], vmem),
-        skip=(skip_gain[None], vmem),
-        router=(router_weight.T, vmem),
-        gate_hbm=(gate_weight, hbm),
-        up_hbm=(up_weight, hbm),
-        down_hbm=(down_weight, hbm),
-        out_grad=(out_grad, vmem),
-    )
+    loaded = dict(
+        tokens=tokens,
+        routes=routes.T,
+        dt=dt_raw.T,
+        b_proj=b_proj.T,
+        c_proj=c_proj.T,
+        rate=decay_rate[None],
+        skip=skip_gain[None],
+        router=router_weight.T,
+        out_grad=out_grad,
+    )
+    given = {name + HBM: array for name, array in loaded.items()}
+    given.update(gate_hbm=gate_weight, up_hbm=up_weight, down_hbm=down_weight)
     made = dict(
         block_out=((count, width), HALF),
         token_grad=((count, width), HALF),
         gate_grad=((features, units), HALF),
         up_grad=((features, units), HALF),
-        down_grad=((units, features), HALF),
         router_grad=((experts, width), FULL),
-        small=((8, 128), FULL),
+        rate_grad=((1, heads), FULL),
+        skip_grad=((1, heads), FULL),
+        hidden2=((total, units), HALF),
+        grads=((total, features), HALF),
     )
     if fused:
         split = dict(
@@ -791,19 +862,18 @@
         split,
         down_w=((units, features), HALF),
         rows=((total, features), HALF),
-        grads=((total, features), HALF),
         send_rows=((total, width), HALF),
         send_grads=((total, width), HALF),
         back_f=((total, width), HALF),
         back_b=((total, width), HALF),
         unit_raw=((total, units), FULL),
         hidden=((total, units), HALF),
-        hidden2=((total, units), HALF),
         away=((2, chip_count, total, width), HALF),
         mine=((2, chip_count, total, width), HALF),
         pair=((2, chip_count, total, width), HALF),
-        chips=((2, chip_count, total, width), HALF),
+        chips=((2, chip_count - 1, total, width), HALF),
         summed=((2, total, width), HALF),
+        held=((total, width), FULL),
         table=((total, 2 * count), FULL),
         across=((2 * count, total), HALF),
         normed=((count, width), FULL),
@@ -816,7 +886,7 @@
         stack=((heads * count, width), FULL),
         slot_weight=((total, 128), FULL),
         slot_scale=((total, 128), FULL),
-        values=((total, 128), FULL),
+        values=((total, 256), FULL),
         slot_src=((blocks, 8, 128), FULL),
         slot_all=((blocks, 8, 128), FULL),
         value_src=((blocks, 8, 128), FULL),
@@ -833,27 +903,30 @@
         last=(DP, (8, count)),
         small=(EXPERT, (8, 128)),
     )
-    counts = dict(slot=blocks, value=blocks)
+    sems = dict(slot_sems=dma((2,)), value_sems=dma((2,)))
     for name, (axis, shape) in exchanged.items():
-        counts[name] = lax.axis_size(axis)
         scratch[name + SRC] = (shape, FULL)
-        scratch[name + ALL] = ((counts[name],) + shape, FULL)
-    shapes = {name: (amount,) for name, amount in counts.items()}
-    shapes.update(
-        z=(2, blocks),
-        c=(2, blocks * chip_count),
-        p=(2, blocks * chip_count),
+        scratch[name + ALL] = ((lax.axis_size(axis),) + shape, FULL)
+        sems[name + SEMS] = dma((2,))
+    for name, array in loaded.items():
+        scratch[name] = (array.shape, array.dtype)
+    shapes = dict(
+        z=(2, blocks - 1),
+        c=(2, chip_count - 1, blocks),
+        p=(2, chip_count),
         pair=(2, chip_count),
-        chip=(2, chip_count),
-        back=(2, blocks),
-    )
-    sems = {name + way: dma(shape) for name, shape in shapes.items() for way in (SEND, RECV)}
-    sems.update(local_sem=dma((2,)), weight_sem=dma((3,)))
+        chip=(2, chip_count - 1),
+        back=(2,),
+    )
+    for name, shape in shapes.items():
+        sems[name + SEND] = dma((2,))
+        sems[name + RECV] = dma(shape)
+    sems.update(local_sem=dma((2,)), weight_sem=dma((3,)), load_sem=dma((len(loaded),)))
     names = [*given, *made, *scratch, *sems]
-    block_out, token_grad, gate_part, up_part, down_part, router_part, small = pl.pallas_call(
-        functools.partial(step_kernel, names, capacity, cap, fused),
+    results = pl.pallas_call(
+        functools.partial(step_kernel, names, list(loaded), capacity, cap, fused),
         out_shape=[jax.ShapeDtypeStruct(shape, kind) for shape, kind in made.values()],
-        in_specs=[spec for _, spec in given.values()],
+        in_specs=[hbm] * len(given),
         out_specs=[vmem] * len(made),
         scratch_shapes=[pltpu.VMEM(shape, kind) for shape, kind in scratch.values()]
         + list(sems.values()),
@@ -861,7 +934,18 @@
             collective_id=7, has_side_effects=True, vmem_limit_bytes=40 << 20
         ),
         name="step",
-    )(*[array for array, _ in given.values()])
+    )(*[pltpu.with_memory_space_constraint(x, pltpu.HBM) for x in given.values()])
+    *ready, hidden, grads = results
+    shapes = [*ready, jax.ShapeDtypeStruct((units, features), HALF)]
+    block_out, token_grad, gate_part, up_part, router_part, rate, skip, down_part = pl.pallas_call(
+        write_kernel,
+        out_shape=[jax.ShapeDtypeStruct(like.shape, like.dtype) for like in shapes],
+        in_specs=[vmem] * len(results),
+        out_specs=[hbm] * len(shapes),
+        scratch_shapes=[pltpu.VMEM((units, features), HALF), dma((len(shapes) * PIECES,))],
+        compiler_params=pltpu.CompilerParams(vmem_limit_bytes=12 << 20),
+        name="write",
+    )(hidden, grads, *ready)
     return (
         block_out,
         token_grad,
@@ -869,8 +953,8 @@
         up_part[None],
         down_part[None],
         router_part.T,
-        small[0, :heads],
-        small[1, :heads],
+        rate[0],
+        skip[0],
     )
 
 

time: 84.5 us -> 60.9 us (0.72)
  local copies, waits for them, and re-layouts: 14.3 us -> 0 us
  Pallas kernels: 69.1 us -> 60.1 us
    unnamed x24 -> x0, local copies, waits for them, and re-layouts: 13.8 us -> none
    pallas_call x1 -> x2, Pallas kernels: 69.1 us -> 60.1 us  [the longest x1 55.7 us: body(): pl.pallas_call(functools.partial(step_kernel, names, list(loaded), capaci...]
where the time goes in v2:
time: 60.9 us; the launch traced here: 60.8 us
  Pallas kernels  60.1 us (99%)
  between operations  0.65 us (1%)
    pallas_call x1, Pallas kernels, body(): pl.pallas_call(functools.partial(step_kernel, names, list(loaded), capaci...  55.7 us
    pallas_call x1, Pallas kernels, body(): pl.pallas_call(write_kernel, out_shape=[jax.ShapeDtypeStruct(like.shape,...  4.42 us

profile of v2, /device:TPU:0, one launch (start us, length us, event | category | flops | bytes accessed | tf_op | source)
XLA Modules:
  0.0 60.8 jit_solution(5549958706929081025)
XLA Ops:
  0.6 55.7 %step.1 = (bf16[128,256]{1,0:T(8,128)(2,1)S(1)}, bf16[128,256]{1,0:T(8,128)(2,1)S(1)}, bf16[2048,896]{1,0:T(8,128)(2,1)S(1)}, bf16[2048,896]{1,0:T(8,128)(2,1)S(...) custom-call(bf16[128,256]{1,0:T(8,128)(2,1)} %refs_0_.1, ...), custom_call_target="tpu_custom_call" | custom-call | tf_op jit(solution)/shard_map/step/pallas_call | solution.py:926
  56.3 4.4 %write.1 = (bf16[128,256]{1,0:T(8,128)(2,1)}, bf16[128,256]{1,0:T(8,128)(2,1)}, bf16[2048,896]{1,0:T(8,128)(2,1)}, bf16[2048,896]{1,0:T(8,128)(2,1)}, f32[4,256]...) custom-call(bf16[320,896]{1,0:T(8,128)(2,1)S(1)} %get-tuple-element.25.hidden, ...), custom_call_target="tpu_custom_call" | custom-call | tf_op jit(solution)/shard_map/write/pallas_call | solution.py:940

commit v3 on v2

--- a/solution.py
+++ b/solution.py
@@ -185,6 +185,7 @@
         start, arrive, sent = exchange(axis, lambda _: src, everyone, getattr(r, name + SEMS))
 
         def launch(value):
+            value = value.astype(src.dtype)
             src[...] = value
             start()
             everyone[place if axis == DP else block] = value
@@ -230,7 +231,7 @@
             src_ref=cut,
             dst_ref=cut,
             send_sem=r.c_send.at[t],
-            recv_sem=r.c_recv.at[t, way, k],
+            recv_sem=r.u_recv.at[k] if (t, way) == (0, 0) else r.c_recv.at[t, way],
             device_id={DP: 2 * to + core},
             device_id_type=MESH,
         )
@@ -268,14 +269,17 @@
 
     def from_chip(t, way):
         owner = 2 * chip_from(way) + core
-
-        def one(k):
-            spread_copy(t, k, way, owner, chip_to(way)).wait_recv()
-            if square and t == 0 and way == 0:
-                spread_copy(t, k, 2, owner, chip_to(1)).start()
-
-        loop(blocks, one)
+        cut = wholes[t].at[:, columns(owner)]
+        waits(cut, (r.c_send.at[t], r.c_recv.at[t, way]))[0]()
         partner_copy(t, way, owner).start()
+
+    def relay(k):
+        owner = 2 * chip_from(0) + core
+        spread_copy(0, k, 0, owner, chip_to(0)).wait_recv()
+        if square:
+            spread_copy(0, k, 2, owner, chip_to(1)).start()
+        if k == blocks - 1:
+            partner_copy(0, 0, owner).start()
 
     def from_partner(t, way):
         partner_copy(t, way, 2 * partner_chip(way) + 1 - core).wait_recv()
@@ -300,6 +304,16 @@
             device_id_type=MESH,
         )
 
+    def piece_copy(t, way, n, c, to):
+        return pltpu.make_async_remote_copy(
+            src_ref=mine.at[t, c, strip(ahead(n + 1))],
+            dst_ref=chips.at[t, way, strip(ahead(n + 1))],
+            send_sem=r.chip_send.at[t],
+            recv_sem=r.piece_recv.at[t, way // 2, n],
+            device_id={DP: 2 * to + core},
+            device_id_type=MESH,
+        )
+
     def back_copy(t, k, land):
         return pltpu.make_async_remote_copy(
             src_ref=summed.at[t, strip(ahead(k)), :],
@@ -310,14 +324,13 @@
             device_id_type=MESH,
         )
 
-    def tiles(t, term, between=None):
+    def tiles(t, term, when, between):
         def settle(c):
             pair_copy(t, c).wait_recv()
             mine[t, c] = (r.held[...] + pair[t, c].astype(FULL)).astype(HALF)
 
         def step(q):
-            if between is not None:
-                pl.when(q == 2)(between)
+            pl.when(q == when)(between)
             value = term(chip_in_turn(q))
             left, right = (value[:, :width], value[:, width:])
             away[t, chip_in_turn(q)] = jnp.where(core == 0, right, left).astype(HALF)
@@ -328,11 +341,14 @@
                 c = chip_in_turn(q - 1)
                 settle(c)
                 if square:
-                    for way, when in ((0, 1), (1, 2 + core)):
-
-                        @pl.when(q == when)
-                        def _():
-                            chip_copy(t, way, c, chip_to(0)).start()
+
+                    @pl.when(q == 1)
+                    def _():
+                        loop(blocks, lambda n: piece_copy(t, 0, n, c, chip_to(0)).start())
+
+                    @pl.when(q == 2 + core)
+                    def _():
+                        chip_copy(t, 1, c, chip_to(0)).start()
                 else:
                     chip_copy(t, q - 1, c, c).start()
 
@@ -344,17 +360,35 @@
     def combine(t):
         if square:
             c = chip_to(1)
-            chip_copy(t, 0, c, c).wait_recv()
-            mine[t, c] = (mine[t, c].astype(FULL) + chips[t, 0].astype(FULL)).astype(HALF)
-            chip_copy(t, 2, c, c).start()
+
+            def one(n):
+                piece_copy(t, 0, n, c, c).wait_recv()
+                row = strip(ahead(n + 1))
+                value = mine[t, c, row].astype(FULL) + chips[t, 0, row].astype(FULL)
+                mine[t, c, row] = value.astype(HALF)
+                piece_copy(t, 2, n, c, c).start()
+
+            loop(blocks, one)
 
     def finish(t):
-        value = mine[t, chip].astype(FULL)
-        for way in range(1 if square else 0, chip_count - 1):
+        wholes_in = (1,) if square else range(chip_count - 1)
+        for way in wholes_in:
             chip_copy(t, way, chip, chip_to(way)).wait_recv()
-            value = value + chips[t, way].astype(FULL)
-        summed[t] = value.astype(HALF)
-        loop(blocks - 1, lambda k: back_copy(t, k + 1, block).start())
+
+        def one(n):
+            row = strip(ahead(n + 1))
+            value = mine[t, chip, row].astype(FULL)
+            if square:
+                piece_copy(t, 2, n, chip, chip).wait_recv()
+            for way in range(1 if square else 0, chip_count - 1):
+                value = value + chips[t, way, row].astype(FULL)
+            summed[t, row] = value.astype(HALF)
+
+            @pl.when(n < blocks - 1)
+            def _():
+                back_copy(t, n + 1, block).start()
+
+        loop(blocks, one)
         backs[t][strip(block), :] = summed[t, strip(block), :]
 
     def backs_arrive(t):
@@ -463,7 +497,7 @@
         for k in range(blocks):
             at = blocks - 1 - k if reverse else k
             reach = at > block if reverse else at < block
-            held = jnp.where(reach, r.decay_all[at][0:1, :] * held + states[at], held)
+            held = jnp.where(reach, r.decay_all[at][0:1, :] * held + states[at].astype(FULL), held)
         return held
 
     state_in = carry(r.state_all, False)
@@ -484,6 +518,32 @@
     pass_on(0)
     for way in range(chip_count - 1):
         from_chip(1, way)
+    weights[1].wait()
+    weights[2].wait()
+    for held in gu_s:
+        held[...] = jnp.zeros_like(held)
+
+    def chunk(d):
+        for held, weight in zip(gu_s, gu_w):
+            held[...] += fast(rows[:, columns(d)], weight[columns(d), :])
+
+    chunk(place)
+    relay(0)
+    from_partner(0, -1)
+    chunk(2 * chip + 1 - core)
+    early = blocks // 2
+    for k in range(1, early):
+        relay(k)
+    for way in range(-1, chip_count - 1):
+        from_partner(1, way)
+    weights[0].wait()
+    cut_list = slices(units, 256)
+    for n in range(max(len(cut_list), blocks - early)):
+        if early + n < blocks:
+            relay(early + n)
+        if n < len(cut_list):
+            at, span = cut_list[n]
+            r.unit_raw[:, at : at + span] = fast(grads[...], down_w[at : at + span, :], NT)
 
     stat_arrive()
     stats = jnp.sum(r.stat_all[...], axis=0)
@@ -505,22 +565,18 @@
         r.slot_src[e, :, :cap] = slot_wide[:, e * cap : (e + 1) * cap]
     slot_start()
     r.slot_all[block] = r.slot_src[block]
-    weights[1].wait()
-    weights[2].wait()
-    for held in gu_s:
-        held[...] = jnp.zeros_like(held)
-
-    def chunk(d):
-        for held, weight in zip(gu_s, gu_w):
-            held[...] += fast(rows[:, columns(d)], weight[columns(d), :])
-
-    chunk(place)
-    from_chip(0, 0)
-    for way in range(-1, chip_count - 1):
-        from_partner(1, way)
-    weights[0].wait()
-    for at, span in slices(units, 256):
-        r.unit_raw[:, at : at + span] = fast(grads[...], down_w[at : at + span, :], NT)
+    chunk(2 * chip_from(0) + core)
+    for way in range(1, chip_count - 1):
+        from_chip(0, way)
+        from_partner(0, way - 1)
+
+        def one(n):
+            other = 2 * partner_chip(way - 1) + 1 - core
+            chunk((1 - n) * other + n * (2 * chip_from(way) + core))
+
+        loop(2, one)
+    from_partner(0, chip_count - 2)
+    chunk(2 * partner_chip(chip_count - 2) + 1 - core)
 
     slot_arrive()
     pick = (iota((8, 256), 0) // 2 == iota((8, 256), 1) // 128).astype(HALF)
@@ -529,19 +585,6 @@
     for j, wide in enumerate(wides):
         r.slot_weight[j * cap : (j + 1) * cap, :] = wide[:cap, :128]
         r.slot_scale[j * cap : (j + 1) * cap, :] = wide[:cap, 128:]
-
-    for way in range(chip_count - 1):
-        if way > 0:
-            from_chip(0, way)
-        from_partner(0, way - 1)
-
-        def one(n):
-            other = 2 * partner_chip(way - 1) + 1 - core
-            chunk((1 - n) * other + n * (2 * chip_from(way) + core))
-
-        loop(2, one)
-    from_partner(0, chip_count - 2)
-    chunk(2 * partner_chip(chip_count - 2) + 1 - core)
 
     tall = 16
     r.values[...] = jnp.zeros_like(r.values)
@@ -608,19 +651,6 @@
     def output_term(c):
         return fast(r.hidden[...], down_w[:, both_columns(c)])
 
-    tiles(1, input_term, send_values)
-
-    combine(1)
-    value_arrive()
-    inner_part = jnp.zeros((8, 2 * count), FULL)
-    for j in range(blocks):
-        inner_part = inner_part + exact(
-            r.value_all[j, :, :cap], r.table[j * cap : (j + 1) * cap, :]
-        )
-    inner_launch(inner_part)
-
-    tiles(0, output_term)
-
     wide_cut = 256
 
     def weight_grads(lo, hi):
@@ -638,9 +668,19 @@
 
     cuts = features // wide_cut
 
-    finish(1)
-    weight_grads(0, cuts // 2)
-    combine(0)
+    tiles(1, input_term, 2, send_values)
+
+    combine(1)
+    value_arrive()
+    inner_part = jnp.zeros((8, 2 * count), FULL)
+    for j in range(blocks):
+        inner_part = inner_part + exact(
+            r.value_all[j, :, :cap], r.table[j * cap : (j + 1) * cap, :]
+        )
+    inner_launch(inner_part)
+
+    tiles(0, output_term, chip_count - 1, lambda: finish(1))
+    weight_grads(0, cuts // 4)
     inner_arrive()
     inner_all = jnp.sum(r.inner_all[...], axis=0)
     gap_grad = first_weight * second_weight * (inner_all[0:1, :count] - inner_all[0:1, count:])
@@ -670,6 +710,7 @@
     resid_grad = r.base[...] + scale_two * moe_grad
     r.resid_grad[...] = resid_grad
     sgrad_launch(exact(c_side, grow_wide * resid_grad))
+    combine(0)
     normed = r.normed[...]
     pairing_back = exact(b_side, c_side, TN)
     upper = iota((count, count), 0) <= iota((count, count), 1)
@@ -693,10 +734,8 @@
     local_grad = step_wide * exact(r.mixing[...], r.stack[...]) + skip_wide * resid_grad
     skip_lanes = jnp.sum(resid_grad * normed, axis=0, keepdims=True)
     rate_lanes = jnp.sum(resid_grad * r.carried[...] * sum_wide, axis=0, keepdims=True)
-    weight_grads(cuts // 2, 5 * cuts // 8)
+    weight_grads(cuts // 4, 5 * cuts // 8)
     finish(0)
-    weight_grads(5 * cuts // 8, cuts)
-
 
     sgrad_arrive()
     state_grad = carry(r.sgrad_all, True)
@@ -717,6 +756,7 @@
     small_part = jnp.where(row128 == 0, -(small_part + rate_parts), small_part)
     small_launch(small_part)
 
+    weight_grads(5 * cuts // 8, cuts)
     backs_arrive(0)
     first_out = fast(r.across[:count, :], backs[0][...])
     second_out = fast(r.across[count:, :], backs[0][...])
@@ -755,7 +795,7 @@
     for t in range(2):
         for ref, send, recv in (
             (sources[t].at[:lead], r.z_send, r.z_recv.at[t, 0]),
-            (wholes[t].at[:, : (chip_count - 1) * width], r.c_send, r.c_recv.at[t, 0, 0]),
+            (wholes[t].at[:, : (chip_count - 1) * width], r.c_send, r.c_recv.at[t, 0]),
             (wholes[t].at[:, : chip_count * width], r.p_send, r.p_recv.at[t, 0]),
             (away.at[t], r.pair_send, r.pair_recv.at[t, 0]),
             (mine.at[t, 1:], r.chip_send, r.chip_recv.at[t, 0]),
@@ -905,14 +945,15 @@
     )
     sems = dict(slot_sems=dma((2,)), value_sems=dma((2,)))
     for name, (axis, shape) in exchanged.items():
-        scratch[name + SRC] = (shape, FULL)
-        scratch[name + ALL] = ((lax.axis_size(axis),) + shape, FULL)
+        kind = HALF if shape == (state, width) else FULL
+        scratch[name + SRC] = (shape, kind)
+        scratch[name + ALL] = ((lax.axis_size(axis),) + shape, kind)
         sems[name + SEMS] = dma((2,))
     for name, array in loaded.items():
         scratch[name] = (array.shape, array.dtype)
     shapes = dict(
         z=(2, blocks - 1),
-        c=(2, chip_count - 1, blocks),
+        c=(2, chip_count - 1),
         p=(2, chip_count),
         pair=(2, chip_count),
         chip=(2, chip_count - 1),
@@ -921,7 +962,7 @@
     for name, shape in shapes.items():
         sems[name + SEND] = dma((2,))
         sems[name + RECV] = dma(shape)
-    sems.update(local_sem=dma((2,)), weight_sem=dma((3,)), load_sem=dma((len(loaded),)))
+    sems.update(local_sem=dma((2,)), weight_sem=dma((3,)), load_sem=dma((len(loaded),)), u_recv=dma((blocks,)), piece_recv=dma((2, 2, blocks)))
     names = [*given, *made, *scratch, *sems]
     results = pl.pallas_call(
         functools.partial(step_kernel, names, list(loaded), capacity, cap, fused),

time: 60.9 us -> 59.7 us (0.980)
  Pallas kernels: 60.1 us -> 58.9 us
    pallas_call x1, Pallas kernels: 55.7 us -> 54.5 us  [body(): pl.pallas_call(functools.partial(step_kernel, names, list(loaded), capaci...]
where the time goes in v3:
time: 59.7 us; the launch traced here: 59.6 us
  Pallas kernels  58.9 us (99%)
  between operations  0.65 us (1%)
    pallas_call x1, Pallas kernels, body(): pl.pallas_call(functools.partial(step_kernel, names, list(loaded), capaci...  54.5 us
    pallas_call x1, Pallas kernels, body(): pl.pallas_call(write_kernel, out_shape=[jax.ShapeDtypeStruct(like.shape,...  4.42 us

profile of v3, /device:TPU:0, one launch (start us, length us, event | category | flops | bytes accessed | tf_op | source)
XLA Modules:
  0.0 59.6 jit_solution(3504264668101617690)
XLA Ops:
  0.6 54.5 %step.1 = (bf16[128,256]{1,0:T(8,128)(2,1)S(1)}, bf16[128,256]{1,0:T(8,128)(2,1)S(1)}, bf16[2048,896]{1,0:T(8,128)(2,1)S(1)}, bf16[2048,896]{1,0:T(8,128)(2,1)S(...) custom-call(bf16[128,256]{1,0:T(8,128)(2,1)} %refs_0_.1, ...), custom_call_target="tpu_custom_call" | custom-call | tf_op jit(solution)/shard_map/step/pallas_call | solution.py:967
  55.1 4.4 %write.1 = (bf16[128,256]{1,0:T(8,128)(2,1)}, bf16[128,256]{1,0:T(8,128)(2,1)}, bf16[2048,896]{1,0:T(8,128)(2,1)}, bf16[2048,896]{1,0:T(8,128)(2,1)}, f32[4,256]...) custom-call(bf16[320,896]{1,0:T(8,128)(2,1)S(1)} %get-tuple-element.25.hidden, ...), custom_call_target="tpu_custom_call" | custom-call | tf_op jit(solution)/shard_map/write/pallas_call | solution.py:981

commit v4 on v3

--- a/solution.py
+++ b/solution.py
@@ -531,20 +531,6 @@
     relay(0)
     from_partner(0, -1)
     chunk(2 * chip + 1 - core)
-    early = blocks // 2
-    for k in range(1, early):
-        relay(k)
-    for way in range(-1, chip_count - 1):
-        from_partner(1, way)
-    weights[0].wait()
-    cut_list = slices(units, 256)
-    for n in range(max(len(cut_list), blocks - early)):
-        if early + n < blocks:
-            relay(early + n)
-        if n < len(cut_list):
-            at, span = cut_list[n]
-            r.unit_raw[:, at : at + span] = fast(grads[...], down_w[at : at + span, :], NT)
-
     stat_arrive()
     stats = jnp.sum(r.stat_all[...], axis=0)
     scale_row = lax.rsqrt(stats[0:1] / features + EPSILON)
@@ -565,8 +551,33 @@
         r.slot_src[e, :, :cap] = slot_wide[:, e * cap : (e + 1) * cap]
     slot_start()
     r.slot_all[block] = r.slot_src[block]
+    early = blocks // 2
+    for k in range(1, early):
+        relay(k)
+    for way in range(-1, chip_count - 1):
+        from_partner(1, way)
+    weights[0].wait()
+    cut_list = slices(units, 256)
+    for n in range(max(len(cut_list), blocks - early)):
+        if early + n < blocks:
+            relay(early + n)
+        if n < len(cut_list):
+            at, span = cut_list[n]
+            r.unit_raw[:, at : at + span] = fast(grads[...], down_w[at : at + span, :], NT)
+
+    def take_slots():
+        slot_arrive()
+        pick = (iota((8, 256), 0) // 2 == iota((8, 256), 1) // 128).astype(HALF)
+
+        wides = [fast(r.slot_all[j].astype(HALF), pick, TN) for j in range(blocks)]
+        for j, wide in enumerate(wides):
+            r.slot_weight[j * cap : (j + 1) * cap, :] = wide[:cap, :128]
+            r.slot_scale[j * cap : (j + 1) * cap, :] = wide[:cap, 128:]
+
     chunk(2 * chip_from(0) + core)
     for way in range(1, chip_count - 1):
+        if way == chip_count - 2:
+            take_slots()
         from_chip(0, way)
         from_partner(0, way - 1)
 
@@ -577,14 +588,6 @@
         loop(2, one)
     from_partner(0, chip_count - 2)
     chunk(2 * partner_chip(chip_count - 2) + 1 - core)
-
-    slot_arrive()
-    pick = (iota((8, 256), 0) // 2 == iota((8, 256), 1) // 128).astype(HALF)
-
-    wides = [fast(r.slot_all[j].astype(HALF), pick, TN) for j in range(blocks)]
-    for j, wide in enumerate(wides):
-        r.slot_weight[j * cap : (j + 1) * cap, :] = wide[:cap, :128]
-        r.slot_scale[j * cap : (j + 1) * cap, :] = wide[:cap, 128:]
 
     tall = 16
     r.values[...] = jnp.zeros_like(r.values)

time: 59.7 us -> 59.4 us (level)
  no operation moved by 1% of the time
where the time goes in v4:
time: 59.4 us; the launch traced here: 59.2 us
  Pallas kernels  58.5 us (98%)
  between operations  0.65 us (1%)
    pallas_call x1, Pallas kernels, body(): pl.pallas_call(functools.partial(step_kernel, names, list(loaded), capaci...  54.1 us
    pallas_call x1, Pallas kernels, body(): pl.pallas_call(write_kernel, out_shape=[jax.ShapeDtypeStruct(like.shape,...  4.42 us

profile of v4, /device:TPU:0, one launch (start us, length us, event | category | flops | bytes accessed | tf_op | source)
XLA Modules:
  0.0 59.2 jit_solution(3194767007472146278)
XLA Ops:
  0.6 54.1 %step.1 = (bf16[128,256]{1,0:T(8,128)(2,1)S(1)}, bf16[128,256]{1,0:T(8,128)(2,1)S(1)}, bf16[2048,896]{1,0:T(8,128)(2,1)S(1)}, bf16[2048,896]{1,0:T(8,128)(2,1)S(...) custom-call(bf16[128,256]{1,0:T(8,128)(2,1)} %refs_0_.1, ...), custom_call_target="tpu_custom_call" | custom-call | tf_op jit(solution)/shard_map/step/pallas_call | solution.py:970
  54.8 4.4 %write.1 = (bf16[128,256]{1,0:T(8,128)(2,1)}, bf16[128,256]{1,0:T(8,128)(2,1)}, bf16[2048,896]{1,0:T(8,128)(2,1)}, bf16[2048,896]{1,0:T(8,128)(2,1)}, f32[4,256]...) custom-call(bf16[320,896]{1,0:T(8,128)(2,1)S(1)} %get-tuple-element.25.hidden, ...), custom_call_target="tpu_custom_call" | custom-call | tf_op jit(solution)/shard_map/write/pallas_call | solution.py:984
